TPU v7x, 16 devices: a whole 2x2x2 slice. The times are simulated.
16 devices in a mesh: dp: 4 (over z, y), tp: 4 (over x, core).
Axes of the slice: x: 2, y: 2, z: 2, core: 2. Of those that a mesh axis runs over, the one named last changes fastest.
Arguments:
- x: bfloat16 [512, 2560], P('dp'), parts along dimension 0
- ln_attn_gamma: float32 [2560], replicated
- ln_attn_beta: float32 [2560], replicated
- ln_mlp_gamma: float32 [2560], replicated
- ln_mlp_beta: float32 [2560], replicated
- w_qkv: bfloat16 [2560, 32, 3, 80], P(None, 'tp')
- w_out: bfloat16 [32, 1, 80, 2560], P('tp')
- w_up: bfloat16 [2560, 10240], P(None, 'tp')
- w_down: bfloat16 [10240, 2560], P('tp')
- k_cache: bfloat16 [512, 32, 128, 80], P('dp', 'tp'), parts along dimension 0
- v_cache: bfloat16 [512, 32, 128, 80], P('dp', 'tp'), parts along dimension 0
- positions: int32 [512], P('dp'), parts along dimension 0
Outputs:
- output 1: bfloat16 [512, 2560], P('dp'), parts along dimension 0
- output 2: bfloat16 [512, 32, 128, 80], P('dp', 'tp'), parts along dimension 0
- output 3: bfloat16 [512, 32, 128, 80], P('dp', 'tp'), parts along dimension 0
There are 4 independent parts. A program takes and returns all parts, laid end to end along the dimension named above; an argument that names none is the same for every part.
All inputs are finite; a program needn't handle non-finite values.
Results may differ from a plain program's by a relative error of at most 0.0101179.
Values are sent between devices in bfloat16 or wider.
A program may use at most 1 GiB of HBM per device.

v0:
```python
import jax
import jax.numpy as jnp
from jax import lax
from jax.sharding import PartitionSpec as P

LN_EPS = 1e-5
ROPE_BASE = 10000.0
NEG_BIG = -1e30


def layer_norm(act_rows, ln_gamma, ln_beta):
    rows_f32 = act_rows.astype(jnp.float32)
    row_mean = jnp.mean(rows_f32, axis=-1, keepdims=True)
    centred = rows_f32 - row_mean
    row_var = jnp.mean(centred * centred, axis=-1, keepdims=True)
    return (centred * lax.rsqrt(row_var + LN_EPS) * ln_gamma + ln_beta).astype(jnp.bfloat16)


def apply_rotary(vectors, cos_t, sin_t):
    half_width = vectors.shape[-1] // 2
    as_f32 = vectors.astype(jnp.float32)
    lower_half = as_f32[..., :half_width]
    upper_half = as_f32[..., half_width:]
    return jnp.concatenate([lower_half * cos_t - upper_half * sin_t, upper_half * cos_t + lower_half * sin_t], axis=-1).astype(jnp.bfloat16)


def attend_local(attn_in, w_qkv, k_cache, v_cache, positions):
    n_query = w_qkv.shape[2] - 2
    head_dim = w_qkv.shape[3]
    qkv_rows = jnp.einsum('bd,dgjh->bgjh', attn_in, w_qkv, preferred_element_type=jnp.float32).astype(jnp.bfloat16)
    inv_freq = ROPE_BASE ** (-2.0 * jnp.arange(head_dim // 2, dtype=jnp.float32) / head_dim)
    angles = positions.astype(jnp.float32)[:, None] * inv_freq[None, :]
    cos_t = jnp.cos(angles)
    sin_t = jnp.sin(angles)
    queries = apply_rotary(qkv_rows[:, :, :n_query], cos_t[:, None, None, :], sin_t[:, None, None, :])
    new_key = apply_rotary(qkv_rows[:, :, n_query], cos_t[:, None, :], sin_t[:, None, :])
    new_value = qkv_rows[:, :, n_query + 1]
    slot_ids = jnp.arange(k_cache.shape[2])
    write_mask = (slot_ids[None, :] == positions[:, None])[:, None, :, None]
    keys_all = jnp.where(write_mask, new_key[:, :, None, :], k_cache)
    values_all = jnp.where(write_mask, new_value[:, :, None, :], v_cache)
    valid_mask = (slot_ids[None, :] <= positions[:, None])[:, None, None, :]
    scores = jnp.einsum('bgqh,bgsh->bgqs', queries, keys_all, preferred_element_type=jnp.float32) * (head_dim ** -0.5)
    scores = jnp.where(valid_mask, scores, NEG_BIG)
    attn_probs = jax.nn.softmax(scores, axis=-1).astype(jnp.bfloat16)
    context = jnp.einsum('bgqs,bgsh->bgqh', attn_probs, values_all, preferred_element_type=jnp.float32).astype(jnp.bfloat16)
    return context, keys_all, values_all


def solution(mesh):
    row_spec = P('dp', None)
    vec_spec = P(None)
    cache_spec = P('dp', 'tp', None, None)

    def device_step(x, ln_attn_gamma, ln_attn_beta, ln_mlp_gamma, ln_mlp_beta, w_qkv, w_out, w_up, w_down, k_cache, v_cache, positions):
        attn_in = layer_norm(x, ln_attn_gamma, ln_attn_beta)
        mlp_in = layer_norm(x, ln_mlp_gamma, ln_mlp_beta)
        context, keys_all, values_all = attend_local(attn_in, w_qkv, k_cache, v_cache, positions)
        attn_part = jnp.einsum('bgqh,gqhd->bd', context, w_out, preferred_element_type=jnp.float32).astype(jnp.bfloat16)
        attn_total = lax.psum(attn_part, 'tp')
        hidden = jax.nn.gelu(jnp.dot(mlp_in, w_up, preferred_element_type=jnp.float32), approximate=False).astype(jnp.bfloat16)
        mlp_part = jnp.dot(hidden, w_down, preferred_element_type=jnp.float32).astype(jnp.bfloat16)
        mlp_total = lax.psum(mlp_part, 'tp')
        layer_out = (x.astype(jnp.float32) + attn_total.astype(jnp.float32) + mlp_total.astype(jnp.float32)).astype(jnp.bfloat16)
        return layer_out, keys_all, values_all

    return jax.shard_map(device_step, mesh=mesh, in_specs=(row_spec, vec_spec, vec_spec, vec_spec, vec_spec, P(None, 'tp', None, None), P('tp', None, None, None), P(None, 'tp'), P('tp', None), cache_spec, cache_spec, P('dp')), out_specs=(row_spec, cache_spec, cache_spec), check_vma=False)
```

profile of v0, /device:TPU:0, one launch (start us, length us, event | category | flops | bytes accessed | tf_op | source)
XLA Modules:
  0.0 146.8 jit_solution(2658432342774983457)
XLA Ops:
  7.2 0.0 copy-start
  7.2 0.0 copy-start.3
  7.2 0.0 copy-start.4
  7.2 0.0 all-reduce.3.cloned.1.call-start
  7.2 0.0 copy-start.1
  7.3 0.8 convert_element_type.65
  8.1 1.4 iota_compare_fusion.1
  9.5 1.3 convert_reduce_fusion
  10.8 0.0 copy-start.6
  10.8 1.4 fusion.12
  12.2 0.0 copy-done.3
  12.2 0.0 copy-done.4
  12.3 0.0 copy-done.1
  12.3 5.5 %fusion.37 = f32[128,1920]{0,1:S(1)} fusion(bf16[2560,1920]{0,1:T(8,128)(2,1)} %bitcast.57, bf16[128,2560]{1,0:T(8,128)(2,1)S(1)} %copy-done.1, f32[2560]{0:T(1024)S(1)} %copy-done.3, f32[2560]{0:T(1024)S(1)} %copy-done.4, f32[128]{0:T(128)S(1)} %add_rsqrt_fusion, f32[128]{0:T(128)S(1)} %broadcast_multiply_fusion), kind=kOutput, calls=%fused_computation.47 | convolution fusion | flops 1260257280 | bytes 11490304
  17.7 0.0 copy-done.6
  17.8 0.0 copy-done.8
  17.8 0.1 convert_element_type.63
  17.8 0.7 fusion.87
  18.6 0.2 multiply_cosine_fusion
  18.7 0.7 fusion.92
  19.4 0.7 fusion.91
  20.1 0.7 pad_maximum_fusion
  20.8 1.1 copy.25
  21.9 1.8 %copy.26 = bf16[128,8,80]{2,1,0:T(8,128)(2,1)} copy(bf16[128,8,80]{0,2,1:T(8,128)(2,1)} %get-tuple-element.7) | data formatting | bytes 327680 | tf_op jit(solution)/shard_map/jit(_where)/broadcast_in_dim | solution.py:41
  23.7 1.6 %maximum_bitcast_fusion = bf16[128,8,80,1]{0,2,1,3:T(8,128)(2,1)} fusion(bf16[128,8,40]{0,2,1:T(8,128)(2,1)} %fusion.92, bf16[128,8,40]{0,2,1:T(8,128)(2,1)} %fusion.91), kind=kLoop, calls=%fused_computation.98 | loop fusion | flops 327680 | bytes 327680 | tf_op jit(solution)/shard_map/concatenate | solution.py:24
  25.3 1.9 %copy.27 = bf16[128,8,80,1]{2,3,1,0:T(2,128)(2,1)} copy(bf16[128,8,80,1]{0,2,1,3:T(8,128)(2,1)} %maximum_bitcast_fusion) | data formatting | bytes 327680 | tf_op jit(solution)/shard_map/concatenate | solution.py:24
  27.2 28.0 %broadcast_select_fusion.1 = (bf16[128,8,128,80]{2,3,1,0:T(8,128)(2,1)}, bf16[128,8,128,80]{2,3,1,0:T(8,128)(2,1)}) fusion(bf16[128,8,128,80]{2,3,1,0:T(8,128)(2,1)} %param.21, pred[128,128]{1,0:T(8,128)(4,1)S(1)} %get-tuple-element.16, bf16[128,8,80]{2,1,0:T(8,128)(2,1)S(1)} %copy.25, bf16[128,8,128,80]{2,3,1,0:T(8,128)(2,1)} %param.22, ...), kind=kLoop, calls=%fused_computation.3 | loop fusion | flops 20971520 | bytes 84230144 | tf_op jit(solution)/shard_map/jit(_where)/select_n | solution.py:40
  55.2 0.0 copy-done.2
  55.2 0.0 copy-start.5
  55.2 10.5 %fusion.126 = f32[128,8,1,128]{3,2,1,0:T(1,128)} fusion(bf16[128,8,80,1]{2,3,1,0:T(2,128)(2,1)S(1)} %copy-done.2, bf16[128,8,128,80]{2,3,1,0:T(8,128)(2,1)} %get-tuple-element.11), kind=kOutput, calls=%fused_computation.150 | convolution fusion | flops 20971520 | bytes 21659648 | tf_op jit(solution)/shard_map/bgqh,bgsh->bgqs/dot_general | solution.py:43
  65.8 0.0 copy-done.5
  65.8 1.4 fusion.29
  67.2 15.7 %fusion.81 = bf16[128,8,1,80]{3,2,1,0:T(2,128)(2,1)} fusion(bf16[128,8,128,80]{2,3,1,0:T(8,128)(2,1)} %get-tuple-element.12, bf16[128,8,128,1]{2,1,0,3:T(8,128)(2,1)S(1)} %fusion.29), kind=kOutput, calls=%fused_computation.86 | convolution fusion | flops 20971520 | bytes 21397504 | tf_op jit(solution)/shard_map/bgqs,bgsh->bgqh/dot_general | solution.py:46
  82.9 1.2 copy.30
  84.1 0.0 copy-done
  84.1 0.0 copy-start.7
  84.1 0.0 copy-start.9
  84.2 0.0 copy-start.10
  84.2 0.0 copy-start.11
  84.2 1.5 %fusion.2 = bf16[128,2560]{1,0:T(8,128)(2,1)} fusion(bf16[8,1,80,2560]{3,2,1,0:T(8,128)(2,1)S(1)} %copy-done, bf16[128,8,1,80]{0,3,1,2:T(8,128)(2,1)S(1)} %copy.30), kind=kOutput, calls=%fused_computation.5 | convolution fusion | flops 419758080 | bytes 4096000 | tf_op jit(solution)/shard_map/bgqh,gqhd->bd/dot_general | solution.py:59
  85.7 0.0 copy-done.7
  85.7 0.0 copy-done.9
  85.7 0.0 copy-done.10
  85.7 0.0 copy-done.11
  85.7 13.1 %convolution_convert_fusion = bf16[128,2560]{1,0:T(8,128)(2,1)} fusion(bf16[2560,2560]{1,0:T(8,128)(2,1)} %param.20, bf16[2560,2560]{1,0:T(8,128)(2,1)} %param.19, bf16[128,2560]{1,0:T(8,128)(2,1)} %param.12, f32[2560]{0:T(1024)S(1)} %copy-done.10, f32[2560]{0:T(1024)S(1)} %copy-done.11, f32[128]{0:T(128)S(1)} %copy-done.9, f32[128]{0:T(128)S(1)} %copy-done.7), kind=kOutput, calls=%fused_computation.6 | convolution fusion | flops 3379036160 | bytes 27546624 | tf_op jit(solution)/shard_map/dot_general | solution.py:62
  98.8 0.0 all-reduce.3.cloned.1.call-update
  98.8 38.5 %all-reduce.3.cloned.1.call-done = (bf16[128,2560]{1,0:T(8,128)(2,1)}, bf16[128,2560]{1,0:T(8,128)(2,1)}) async-done(((bf16[128,2560]{1,0:T(8,128)(2,1)}, bf16[128,2560]{1,0:T(8,128)(2,1)}), (bf16[128,2560]{1,0:T(8,128)(2,1)}, bf16[128,2560]{1,0:T(8,128)(2,1)})) %all-reduce.3.cloned.1.call-update) | async-done | bytes 1310736 | tf_op jit(solution)/shard_map/psum | solution.py:63
  137.4 2.6 %fusion.14 = bf16[128,2560]{1,0:T(8,128)(2,1)} fusion(bf16[128,2560]{1,0:T(8,128)(2,1)} %param.12, bf16[128,2560]{1,0:T(8,128)(2,1)} %get-tuple-element.3, bf16[128,2560]{1,0:T(8,128)(2,1)} %get-tuple-element.4), kind=kLoop, calls=%fused_computation.22 | loop fusion | flops 1966080 | bytes 2621440 | tf_op jit(solution)/shard_map/convert_element_type | solution.py:64
  (6 shorter events, 0.1 us)
Async XLA Ops:
  7.2 77.0 %copy-start = (bf16[8,1,80,2560]{3,2,1,0:T(8,128)(2,1)S(1)}, bf16[8,1,80,2560]{3,2,1,0:T(8,128)(2,1)}, u32[]{:S(2)}) copy-start(bf16[8,1,80,2560]{3,2,1,0:T(8,128)(2,1)} %param.18) | copy-start | bytes 9830404
  7.2 5.1 %copy-start.3 = (f32[2560]{0:T(1024)S(1)}, f32[2560]{0:T(1024)}, u32[]{:S(2)}) copy-start(f32[2560]{0:T(1024)} %param.14) | copy-start | bytes 30724
  7.2 5.1 %copy-start.4 = (f32[2560]{0:T(1024)S(1)}, f32[2560]{0:T(1024)}, u32[]{:S(2)}) copy-start(f32[2560]{0:T(1024)} %param.13) | copy-start | bytes 30724
  7.2 130.2 %all-reduce.3.cloned.1.call-start = ((), (), s32[]{:S(2)}) async-start(), calls=%async_computation | async-start | bytes 2621440 | tf_op jit(solution)/shard_map/psum | solution.py:63
  7.2 5.0 %copy-start.1 = (bf16[128,2560]{1,0:T(8,128)(2,1)S(1)}, bf16[128,2560]{1,0:T(8,128)(2,1)}, u32[]{:S(2)}) copy-start(bf16[128,2560]{1,0:T(8,128)(2,1)} %param.12) | copy-start | bytes 1966084
  10.8 7.0 %copy-start.6 = (f32[128]{0:T(128)}, f32[128]{0:T(128)S(1)}, u32[]{:S(2)}) copy-start(f32[128]{0:T(128)S(1)} %broadcast_multiply_fusion) | copy-start | bytes 1540
  12.2 5.5 %copy-start.8 = (f32[128]{0:T(128)}, f32[128]{0:T(128)S(1)}, u32[]{:S(2)}) copy-start(f32[128]{0:T(128)S(1)} %add_rsqrt_fusion) | copy-start | bytes 1540
  27.2 28.0 %copy-start.2 = (bf16[128,8,80,1]{2,3,1,0:T(2,128)(2,1)S(1)}, bf16[128,8,80,1]{2,3,1,0:T(2,128)(2,1)}, u32[]{:S(2)}) copy-start(bf16[128,8,80,1]{2,3,1,0:T(2,128)(2,1)} %copy.27) | copy-start | bytes 491524
  55.2 10.5 %copy-start.5 = (pred[128,128]{1,0:T(8,128)(4,1)S(1)}, pred[128,128]{1,0:T(8,128)(4,1)}, u32[]{:S(2)}) copy-start(pred[128,128]{1,0:T(8,128)(4,1)} %get-tuple-element.15) | copy-start | bytes 49156
  84.1 1.6 %copy-start.7 = (f32[128]{0:T(128)S(1)}, f32[128]{0:T(128)}, u32[]{:S(2)}) copy-start(f32[128]{0:T(128)} %copy-done.6) | copy-start | bytes 1540
  84.1 1.6 %copy-start.9 = (f32[128]{0:T(128)S(1)}, f32[128]{0:T(128)}, u32[]{:S(2)}) copy-start(f32[128]{0:T(128)} %copy-done.8) | copy-start | bytes 1540
  84.2 1.6 %copy-start.10 = (f32[2560]{0:T(1024)S(1)}, f32[2560]{0:T(1024)}, u32[]{:S(2)}) copy-start(f32[2560]{0:T(1024)} %param.16) | copy-start | bytes 30724
  84.2 1.6 %copy-start.11 = (f32[2560]{0:T(1024)S(1)}, f32[2560]{0:T(1024)}, u32[]{:S(2)}) copy-start(f32[2560]{0:T(1024)} %param.15) | copy-start | bytes 30724
Sparse Core Ops, SparseCore 0:
  98.9 38.3 all-reduce.2
where the time goes:
time: 147 us
  matrix products  46.3 us (31%)
  other arithmetic  41.5 us (28%)
  waiting for transfers between devices  38.6 us (26%)
  between operations  14.2 us (10%)
  local copies, waits for them, and re-layouts  6.13 us (4%)
    psum x1, waiting for transfers between devices, device_step(): mlp_total = lax.psum(mlp_part, 'tp')  38.5 us
    select_n x1, other arithmetic, attend_local(): keys_all = jnp.where(write_mask, new_key[:, :, None, :], k_cache)  28 us
    dot_general x1, matrix products, attend_local(): jnp.einsum('bgqs,bgsh->bgqh', attn_probs, values_all, preferred_element_t...  15.7 us
    dot_general x1, matrix products, device_step(): jnp.dot(hidden, w_down, preferred_element_type=jnp.float32)  13.1 us
    dot_general x1, matrix products, attend_local(): jnp.einsum('bgqh,bgsh->bgqs', queries, keys_all, preferred_element_type=j...  10.5 us
    unnamed x1, matrix products  5.48 us
    concatenate x4, other arithmetic, apply_rotary(): jnp.concatenate([lower_half * cos_t - upper_half * sin_t, upper_half * co...  3.62 us
    concatenate x2, local copies, waits for them, and re-layouts, apply_rotary(): jnp.concatenate([lower_half * cos_t - upper_half * sin_t, upper_half * co...  3.04 us
  transfers between devices with their start and end apart: 1, of which 1 were waited for; matrix products, arithmetic and copies ran while one was open for 0% of the time, Pallas kernels for 0%

commit v1 on v0

v1 whole, which is shorter than its diff:
```python
import functools
import numpy as np
import jax
import jax.numpy as jnp
from jax import lax
from jax.experimental import pallas as pl
from jax.experimental.pallas import tpu as pltpu
from jax.sharding import PartitionSpec as P

LN_EPS = 1e-5
ROPE_BASE = 10000.0
NEG_BIG = -1e30
MESH = pl.DeviceIdType.MESH

ROWS = 128
D = 2560
GROUPS = 8
HEAD = 80
HALF = 40
KV = GROUPS * HEAD
SEQ = 128
BLK = 8
NBLK = ROWS // BLK
WCOLS = 512
NW = D // WCOLS
WSLOTS = 3
QSLOTS = 4


def main_kernel(pos_smem, pos_row, inv_freq, ga, ba, gm, bm, x_ref, wq_hbm, wo_hbm, wu_hbm, wd_hbm, k_hbm, v_hbm,
                part_ref, ko_hbm, vo_hbm,
                kbuf, vbuf, wqbuf, wbuf, wobuf, ain, min_, q_sc, kt_sc, vt_sc, h_sc, acc, ctx,
                ksem, vsem, kosem, vosem, wqsem, wsem, wosem):
    f32, bf16 = jnp.float32, jnp.bfloat16

    def wq_copy(g):
        return pltpu.make_async_copy(wq_hbm.at[pl.ds(g * 240, 240)], wqbuf.at[g % QSLOTS], wqsem.at[g % QSLOTS])

    def k_copy(i):
        rows = pl.ds(i * BLK, BLK)
        return pltpu.make_async_copy(k_hbm.at[rows], kbuf.at[rows], ksem.at[i])

    def v_copy(i):
        rows = pl.ds(i * BLK, BLK)
        return pltpu.make_async_copy(v_hbm.at[rows], vbuf.at[rows], vsem.at[i])

    def ko_copy(i):
        rows = pl.ds(i * BLK, BLK)
        return pltpu.make_async_copy(kbuf.at[rows], ko_hbm.at[rows], kosem.at[i])

    def vo_copy(i):
        rows = pl.ds(i * BLK, BLK)
        return pltpu.make_async_copy(vbuf.at[rows], vo_hbm.at[rows], vosem.at[i])

    def w_copy(hbm, c, n):
        cols = pl.ds(pl.multiple_of(c * WCOLS, WCOLS), WCOLS)
        slot = lax.rem(n, WSLOTS)
        return pltpu.make_async_copy(hbm.at[:, cols], wbuf.at[slot], wsem.at[slot])

    for g in range(QSLOTS):
        wq_copy(g).start()

    gav, bav, gmv, bmv = ga[...], ba[...], gm[...], bm[...]

    def ln_body(r, _):
        rows = pl.ds(pl.multiple_of(r * 16, 16), 16)
        xf = x_ref[rows, :].astype(f32)
        mean = jnp.mean(xf, axis=-1, keepdims=True)
        cen = xf - mean
        var = jnp.mean(cen * cen, axis=-1, keepdims=True)
        nrm = cen * lax.rsqrt(var + LN_EPS)
        ain[rows, :] = (nrm * gav + bav).astype(bf16)
        min_[rows, :] = (nrm * gmv + bmv).astype(bf16)
        return 0

    lax.fori_loop(0, ROWS // 16, ln_body, 0)

    angles = inv_freq[...] * pos_row[...].astype(f32)
    cos_t = jnp.cos(angles)
    sin_t = jnp.sin(angles)

    def rotate(u):
        lo, hi = u[:HALF], u[HALF:]
        return jnp.concatenate([lo * cos_t - hi * sin_t, hi * cos_t + lo * sin_t], axis=0)

    for g in range(GROUPS):
        wq_copy(g).wait()
        y = lax.dot_general(wqbuf[g % QSLOTS], ain[...], (((1,), (1,)), ((), ())), preferred_element_type=f32)
        if g + QSLOTS < GROUPS:
            wq_copy(g + QSLOTS).start()
        else:
            j = g + QSLOTS - GROUPS
            k_copy(j).start()
            v_copy(j).start()
            if j < WSLOTS:
                w_copy(wu_hbm, j, j).start()
        y = y.astype(bf16).astype(f32)
        feat = slice(g * HEAD, (g + 1) * HEAD)
        q_sc[feat, :] = rotate(y[:HEAD]).astype(bf16).astype(f32)
        kt_sc[feat, :] = rotate(y[HEAD:2 * HEAD]).astype(bf16).astype(f32)
        vt_sc[feat, :] = y[2 * HEAD:]
    pltpu.make_async_copy(wo_hbm, wobuf, wosem).start()
    qrows = ctx
    for c in range(KV // 128):
        qrows[:, c * 128:(c + 1) * 128] = q_sc[c * 128:(c + 1) * 128, :].T

    lane8 = lax.broadcasted_iota(jnp.int32, (8, KV), 1)
    sub8 = lax.broadcasted_iota(jnp.int32, (8, KV), 0)
    own8 = (lane8 >= sub8 * HEAD) & (lane8 < sub8 * HEAD + HEAD)
    s_lane = lax.broadcasted_iota(jnp.int32, (8, SEQ), 1)
    c_lane = lax.broadcasted_iota(jnp.int32, (KV, SEQ), 1)
    sel = (lax.broadcasted_iota(jnp.int32, (BLK, BLK * 8), 1) // 8
           == lax.broadcasted_iota(jnp.int32, (BLK, BLK * 8), 0)).astype(f32).astype(bf16)
    zero8 = jnp.zeros((8, SEQ), f32)

    def attend(i):
        k_copy(i).wait()
        v_copy(i).wait()
        base = pl.multiple_of(i * BLK, BLK)
        for j in range(BLK):
            b = base + j
            t = pos_smem[b]
            shift = lax.rem(t - b + SEQ, SEQ)
            hit = c_lane == t
            kbuf[b] = jnp.where(hit, pltpu.roll(kt_sc[...], shift, 1).astype(bf16), kbuf[b])
            vbuf[b] = jnp.where(hit, pltpu.roll(vt_sc[...], shift, 1).astype(bf16), vbuf[b])
        ko_copy(i).start()
        vo_copy(i).start()
        picked = []
        for j in range(0, BLK, 2):
            b0, b1 = base + j, base + j + 1
            qs = []
            for b in (b0, b1):
                row = jnp.broadcast_to(qrows[pl.ds(b, 1), :], (8, KV))
                qs.append(jnp.where(own8, row, 0.0))
            qbd = jnp.concatenate(qs, axis=0).astype(bf16)
            kk = jnp.concatenate([kbuf[b0], kbuf[b1]], axis=1)
            s2 = jnp.dot(qbd, kk, preferred_element_type=f32)
            ps = []
            for n, b in enumerate((b0, b1)):
                s = s2[n * 8:n * 8 + 8, n * SEQ:(n + 1) * SEQ] * (HEAD ** -0.5)
                s = jnp.where(s_lane <= pos_smem[b], s, NEG_BIG)
                e = jnp.exp(s - jnp.max(s, axis=-1, keepdims=True))
                ps.append(e / jnp.sum(e, axis=-1, keepdims=True))
            pbd = jnp.concatenate([jnp.concatenate([ps[0], zero8], axis=1),
                                   jnp.concatenate([zero8, ps[1]], axis=1)], axis=0).astype(bf16)
            vv = jnp.concatenate([vbuf[b0], vbuf[b1]], axis=1)
            c2 = lax.dot_general(pbd, vv, (((1,), (1,)), ((), ())), preferred_element_type=f32)
            picked.append(jnp.where(own8, c2[:8], 0.0))
            picked.append(jnp.where(own8, c2[8:], 0.0))
        stack = jnp.concatenate(picked, axis=0).astype(bf16)
        ctx[pl.ds(base, BLK), :] = jnp.dot(sel, stack, preferred_element_type=f32)

        @pl.when(i + 4 < NBLK)
        def _():
            k_copy(i + 4).start()
            v_copy(i + 4).start()

    def up_body(c, _):
        w_copy(wu_hbm, c, c).wait()
        y = jnp.dot(min_[...], wbuf[lax.rem(c, WSLOTS)], preferred_element_type=f32)
        cols = pl.ds(pl.multiple_of(c * WCOLS, WCOLS), WCOLS)
        h_sc[:, cols] = (0.5 * y * (1.0 + lax.erf(y * (0.5 ** 0.5)))).astype(bf16)
        n = c + WSLOTS

        @pl.when(n < NW)
        def _():
            w_copy(wu_hbm, n, n).start()

        @pl.when(n >= NW)
        def _():
            w_copy(wd_hbm, n - NW, n).start()
        attend(c)
        return 0

    def down_body(c, _):
        n = c + NW
        w_copy(wd_hbm, c, n).wait()
        cols = pl.ds(pl.multiple_of(c * WCOLS, WCOLS), WCOLS)
        acc[:, cols] = jnp.dot(h_sc[...], wbuf[lax.rem(n, WSLOTS)], preferred_element_type=f32)

        @pl.when(c + WSLOTS < NW)
        def _():
            w_copy(wd_hbm, c + WSLOTS, n + WSLOTS).start()
        attend(n)
        return 0

    def rest_body(i, _):
        attend(i)
        return 0

    lax.fori_loop(0, NW, up_body, 0)
    lax.fori_loop(0, NW, down_body, 0)
    lax.fori_loop(2 * NW, NBLK, rest_body, 0)

    pltpu.make_async_copy(wo_hbm, wobuf, wosem).wait()
    cb = ctx[...].astype(bf16)

    def out_body(c, _):
        cols = pl.ds(pl.multiple_of(c * WCOLS, WCOLS), WCOLS)
        part_ref[:, cols] = (acc[:, cols] + jnp.dot(cb, wobuf[:, cols], preferred_element_type=f32)).astype(bf16)
        return 0

    lax.fori_loop(0, NW, out_body, 0)

    def drain(i, _):
        ko_copy(i).wait()
        vo_copy(i).wait()
        return 0

    lax.fori_loop(0, NBLK, drain, 0)


def reduce_kernel(part, x_ref, out_ref, near, far, mine, fin, peer_half,
                  s1, r1, s2, r2, s3, r3):
    f32, bf16 = jnp.float32, jnp.bfloat16
    me = lax.axis_index('tp')
    core = lax.rem(me, 2)
    near_id = me + 1 - 2 * core
    far_id = lax.rem(me + 2, 4)
    half = ROWS // 2
    barrier = pltpu.get_barrier_semaphore()
    for peer in (near_id, far_id):
        pl.semaphore_signal(barrier, inc=1, device_id={'tp': peer}, device_id_type=MESH)
    pl.semaphore_wait(barrier, 2)
    mine_rows = pl.ds(pl.multiple_of(core * half, half), half)
    near_rows = pl.ds(pl.multiple_of((1 - core) * half, half), half)
    c1 = pltpu.make_async_remote_copy(part.at[near_rows], near, s1, r1, device_id={'tp': near_id}, device_id_type=MESH)
    c1.start()
    c1.wait()
    mine[...] = (part[mine_rows, :].astype(f32) + near[...].astype(f32)).astype(bf16)
    c2 = pltpu.make_async_remote_copy(mine, far, s2, r2, device_id={'tp': far_id}, device_id_type=MESH)
    c2.start()
    c2.wait()
    fin[...] = (mine[...].astype(f32) + far[...].astype(f32) + x_ref[mine_rows, :].astype(f32)).astype(bf16)
    c3 = pltpu.make_async_remote_copy(fin, peer_half, s3, r3, device_id={'tp': near_id}, device_id_type=MESH)
    c3.start()
    out_ref[mine_rows, :] = fin[...]
    c3.wait()
    out_ref[near_rows, :] = peer_half[...]


def solution(mesh):
    row_spec = P('dp', None)
    vec_spec = P(None)
    cache_spec = P('dp', 'tp', None, None)
    inv = np.power(np.float64(ROPE_BASE), -2.0 * np.arange(HALF, dtype=np.float64) / HEAD).astype(np.float32)
    inv_tab = np.broadcast_to(inv[:, None], (HALF, ROWS)).copy()
    bf16, f32 = jnp.bfloat16, jnp.float32
    sds = jax.ShapeDtypeStruct
    anyspec = pl.BlockSpec(memory_space=pl.ANY)
    vspec = pl.BlockSpec(memory_space=pltpu.VMEM)
    sspec = pl.BlockSpec(memory_space=pltpu.SMEM)
    dma = pltpu.SemaphoreType.DMA

    main = pl.pallas_call(
        main_kernel,
        out_shape=(sds((ROWS, D), bf16), sds((ROWS, KV, SEQ), bf16), sds((ROWS, KV, SEQ), bf16)),
        in_specs=[sspec] + [vspec] * 7 + [anyspec] * 6,
        out_specs=(vspec, anyspec, anyspec),
        scratch_shapes=[
            pltpu.VMEM((ROWS, KV, SEQ), bf16), pltpu.VMEM((ROWS, KV, SEQ), bf16),
            pltpu.VMEM((QSLOTS, 240, D), bf16), pltpu.VMEM((WSLOTS, D, WCOLS), bf16), pltpu.VMEM((KV, D), bf16),
            pltpu.VMEM((ROWS, D), bf16), pltpu.VMEM((ROWS, D), bf16),
            pltpu.VMEM((KV, ROWS), f32), pltpu.VMEM((KV, ROWS), f32), pltpu.VMEM((KV, ROWS), f32),
            pltpu.VMEM((ROWS, D), bf16), pltpu.VMEM((ROWS, D), f32), pltpu.VMEM((ROWS, KV), f32),
            dma((NBLK,)), dma((NBLK,)), dma((NBLK,)), dma((NBLK,)), dma((QSLOTS,)), dma((WSLOTS,)), dma,
        ],
        compiler_params=pltpu.CompilerParams(vmem_limit_bytes=67043328),
        name='layer',
    )
    half = ROWS // 2
    reduce = pl.pallas_call(
        reduce_kernel,
        out_shape=sds((ROWS, D), bf16),
        in_specs=[vspec, vspec],
        out_specs=vspec,
        scratch_shapes=[pltpu.VMEM((half, D), bf16)] * 5 + [dma] * 6,
        compiler_params=pltpu.CompilerParams(collective_id=0, has_side_effects=True, vmem_limit_bytes=16 << 20),
        name='exchange',
    )

    def device_step(x, ga, ba, gm, bm, w_qkv, w_out, w_up, w_down, k_cache, v_cache, positions):
        kt = jnp.swapaxes(k_cache, 2, 3).reshape(ROWS, KV, SEQ)
        vt = jnp.swapaxes(v_cache, 2, 3).reshape(ROWS, KV, SEQ)
        wq = jnp.transpose(w_qkv, (1, 2, 3, 0)).reshape(3 * KV, D)
        wo = w_out.reshape(KV, D)
        part, ko, vo = main(positions, positions.reshape(1, ROWS), jnp.asarray(inv_tab),
                            ga.reshape(1, D), ba.reshape(1, D), gm.reshape(1, D), bm.reshape(1, D),
                            x, wq, wo, w_up, w_down, kt, vt)
        out = reduce(part, x)
        back = lambda c: jnp.swapaxes(c.reshape(ROWS, GROUPS, HEAD, SEQ), 2, 3)
        return out, back(ko), back(vo)

    return jax.shard_map(device_step, mesh=mesh, in_specs=(row_spec, vec_spec, vec_spec, vec_spec, vec_spec, P(None, 'tp', None, None), P('tp', None, None, None), P(None, 'tp'), P('tp', None), cache_spec, cache_spec, P('dp')), out_specs=(row_spec, cache_spec, cache_spec), check_vma=False)
```

time: 147 us -> 73.3 us (0.50)
  Pallas kernels: 0 us -> 64 us
  matrix products: 46.3 us -> 0 us
  other arithmetic: 41.5 us -> 0 us
  waiting for transfers between devices: 38.6 us -> 0 us
  between operations: 14.2 us -> 0.66 us
  local copies, waits for them, and re-layouts: 6.13 us -> 8.25 us
    pallas_call x0 -> x2, Pallas kernels: none -> 64 us  [the longest x1 49.6 us: device_step(): main(positions, positions.reshape(1, ROWS), jnp.asarray(inv_tab), ga.resh...]
    dot_general x4 -> x0, matrix products: 40.8 us -> none  [the longest x1 15.7 us: attend_local(): jnp.einsum('bgqs,bgsh->bgqh', attn_probs, values_all, preferred_element_t...]
    psum x1 -> x0, waiting for transfers between devices: 38.5 us -> none  [device_step(): mlp_total = lax.psum(mlp_part, 'tp')]
    select_n x1 -> x0, other arithmetic: 28 us -> none  [attend_local(): keys_all = jnp.where(write_mask, new_key[:, :, None, :], k_cache)]
    unnamed x1 -> x0, matrix products: 5.48 us -> none
    reshape x0 -> x4, local copies, waits for them, and re-layouts: none -> 5.24 us  [the longest x1 1.31 us: device_step(): ga.reshape(1, D)]
    convert_element_type x4 -> x0, other arithmetic: 4.17 us -> none  [the longest x1 2.55 us: device_step(): (x.astype(jnp.float32) + attn_total.astype(jnp.float32) + mlp_total.astyp...]
    concatenate x4 -> x0, other arithmetic: 3.62 us -> none  [apply_rotary(): jnp.concatenate([lower_half * cos_t - upper_half * sin_t, upper_half * co...]
  transfers between devices with their start and end apart: 1 -> 0, of which waited for: 1 -> 0; matrix products, arithmetic and copies ran while one was open for 0% -> 0% of each run, Pallas kernels for 0% -> 0%
where the time goes in v1:
time: 73.3 us; the launch traced here: 72.9 us
  Pallas kernels  64 us (87%)
  local copies, waits for them, and re-layouts  8.25 us (11%)
    pallas_call x1, Pallas kernels, device_step(): main(positions, positions.reshape(1, ROWS), jnp.asarray(inv_tab), ga.resh...  49.6 us
    pallas_call x1, Pallas kernels, device_step(): out = reduce(part, x)  14.4 us
    unnamed x5, local copies, waits for them, and re-layouts  3.01 us

profile of v1, /device:TPU:0, one launch (start us, length us, event | category | flops | bytes accessed | tf_op | source)
XLA Modules:
  0.0 72.9 jit_solution(11657793030346681976)
XLA Ops:
  0.6 1.3 %reshape.40.ga = f32[1,2560]{1,0:T(1,128)} reshape(f32[2560]{0:T(1024)} %param.14) | data formatting | bytes 20480 | tf_op jit(solution)/shard_map/reshape | solution.py:289
  1.9 1.3 %reshape.41.ba = f32[1,2560]{1,0:T(1,128)} reshape(f32[2560]{0:T(1024)} %param.15) | data formatting | bytes 20480 | tf_op jit(solution)/shard_map/reshape | solution.py:289
  3.3 1.3 %reshape.42.gm = f32[1,2560]{1,0:T(1,128)} reshape(f32[2560]{0:T(1024)} %param.16) | data formatting | bytes 20480 | tf_op jit(solution)/shard_map/reshape | solution.py:289
  4.6 1.3 %reshape.43.bm = f32[1,2560]{1,0:T(1,128)} reshape(f32[2560]{0:T(1024)} %param.17) | data formatting | bytes 20480 | tf_op jit(solution)/shard_map/reshape | solution.py:289
  5.9 49.6 %layer.1 = (bf16[128,2560]{1,0:T(8,128)(2,1)}, bf16[128,640,128]{2,1,0:T(8,128)(2,1)}, bf16[128,640,128]{2,1,0:T(8,128)(2,1)}) custom-call(s32[128]{0:T(128)} %pos_smem.1, s32[1,128]{1,0:T(1,128)} %bitcast.21, f32[40,128]{1,0:T(8,128)} %constant.2.clone.inv_freq, f32[1,2560]{1,0:T(1,128)} %reshape.40.ga, f32[1,2560]{1,0:T(1,128)} %reshape.41.ba, ...), custom_call_target="tpu_custom_call" | custom-call | tf_op jit(solution)/shard_map/layer/pallas_call | solution.py:288
  55.4 0.0 copy-start
  55.5 1.1 %copy-done = bf16[128,2560]{1,0:T(8,128)(2,1)S(1)} copy-done((bf16[128,2560]{1,0:T(8,128)(2,1)S(1)}, bf16[128,2560]{1,0:T(8,128)(2,1)}, u32[]{:S(2)}) %copy-start) | copy-done | bytes 655384
  56.5 0.0 copy-start.1
  56.5 1.1 %copy-done.1 = bf16[128,2560]{1,0:T(8,128)(2,1)S(1)} copy-done((bf16[128,2560]{1,0:T(8,128)(2,1)S(1)}, bf16[128,2560]{1,0:T(8,128)(2,1)}, u32[]{:S(2)}) %copy-start.1) | copy-done | bytes 655384
  57.6 14.4 %exchange.1 = bf16[128,2560]{1,0:T(8,128)(2,1)S(1)} custom-call(bf16[128,2560]{1,0:T(8,128)(2,1)S(1)} %copy-done.1, bf16[128,2560]{1,0:T(8,128)(2,1)S(1)} %copy-done), custom_call_target="tpu_custom_call" | custom-call | tf_op jit(solution)/shard_map/exchange/pallas_call | solution.py:291
  72.0 0.8 %copy.17 = bf16[128,2560]{1,0:T(8,128)(2,1)} copy(bf16[128,2560]{1,0:T(8,128)(2,1)S(1)} %exchange.1) | data formatting | bytes 1310720
Async XLA Ops:
  55.4 1.1 %copy-start = (bf16[128,2560]{1,0:T(8,128)(2,1)S(1)}, bf16[128,2560]{1,0:T(8,128)(2,1)}, u32[]{:S(2)}) copy-start(bf16[128,2560]{1,0:T(8,128)(2,1)} %x_ref.3) | copy-start | bytes 1966084
  56.5 1.1 %copy-start.1 = (bf16[128,2560]{1,0:T(8,128)(2,1)S(1)}, bf16[128,2560]{1,0:T(8,128)(2,1)}, u32[]{:S(2)}) copy-start(bf16[128,2560]{1,0:T(8,128)(2,1)} %get-tuple-element.6.part) | copy-start | bytes 1966084

commit v2 on v1

--- a/solution.py
+++ b/solution.py
@@ -24,17 +24,28 @@
 WCOLS = 512
 NW = D // WCOLS
 WSLOTS = 3
-QSLOTS = 4
-
-
-def main_kernel(pos_smem, pos_row, inv_freq, ga, ba, gm, bm, x_ref, wq_hbm, wo_hbm, wu_hbm, wd_hbm, k_hbm, v_hbm,
-                part_ref, ko_hbm, vo_hbm,
-                kbuf, vbuf, wqbuf, wbuf, wobuf, ain, min_, q_sc, kt_sc, vt_sc, h_sc, acc, ctx,
-                ksem, vsem, kosem, vosem, wqsem, wsem, wosem):
+QROWS = 240
+HALF_ROWS = ROWS // 2
+CUTS = (24, 104)
+
+
+def main_kernel(pos_smem, pos_row, inv_freq, ga, ba, gm, bm, x_hbm, wq_hbm, wo_hbm, wu_hbm, wd_hbm, k_hbm, v_hbm,
+                kbuf, vbuf, send_ref, keep_ref, xh_ref,
+                x_ref, wqbuf, wbuf, ain, min_, q_sc, kt_sc, vt_sc, acc, ctx,
+                ksem, vsem, wqsem, wsem, wosem, xsem):
     f32, bf16 = jnp.float32, jnp.bfloat16
+    h_sc = ain
 
     def wq_copy(g):
-        return pltpu.make_async_copy(wq_hbm.at[pl.ds(g * 240, 240)], wqbuf.at[g % QSLOTS], wqsem.at[g % QSLOTS])
+        rows = pl.ds(g * QROWS, QROWS)
+        return pltpu.make_async_copy(wq_hbm.at[rows], wqbuf.at[rows], wqsem.at[g])
+
+    def wo_copy():
+        return pltpu.make_async_copy(wo_hbm, wqbuf.at[pl.ds(0, KV)], wosem)
+
+    def kv_start(i):
+        k_copy(i).start()
+        v_copy(i).start()
 
     def k_copy(i):
         rows = pl.ds(i * BLK, BLK)
@@ -43,24 +54,23 @@
     def v_copy(i):
         rows = pl.ds(i * BLK, BLK)
         return pltpu.make_async_copy(v_hbm.at[rows], vbuf.at[rows], vsem.at[i])
-
-    def ko_copy(i):
-        rows = pl.ds(i * BLK, BLK)
-        return pltpu.make_async_copy(kbuf.at[rows], ko_hbm.at[rows], kosem.at[i])
-
-    def vo_copy(i):
-        rows = pl.ds(i * BLK, BLK)
-        return pltpu.make_async_copy(vbuf.at[rows], vo_hbm.at[rows], vosem.at[i])
 
     def w_copy(hbm, c, n):
         cols = pl.ds(pl.multiple_of(c * WCOLS, WCOLS), WCOLS)
         slot = lax.rem(n, WSLOTS)
         return pltpu.make_async_copy(hbm.at[:, cols], wbuf.at[slot], wsem.at[slot])
 
-    for g in range(QSLOTS):
+    x_copy = pltpu.make_async_copy(x_hbm, x_ref, xsem)
+    x_copy.start()
+    for g in range(GROUPS):
         wq_copy(g).start()
-
-    gav, bav, gmv, bmv = ga[...], ba[...], gm[...], bm[...]
+    for j in range(WSLOTS):
+        kv_start(j)
+        w_copy(wu_hbm, j, j).start()
+    kv_start(WSLOTS)
+    x_copy.wait()
+
+    gav, bav, gmv, bmv = [r[...].reshape(1, D) for r in (ga, ba, gm, bm)]
 
     def ln_body(r, _):
         rows = pl.ds(pl.multiple_of(r * 16, 16), 16)
@@ -85,21 +95,13 @@
 
     for g in range(GROUPS):
         wq_copy(g).wait()
-        y = lax.dot_general(wqbuf[g % QSLOTS], ain[...], (((1,), (1,)), ((), ())), preferred_element_type=f32)
-        if g + QSLOTS < GROUPS:
-            wq_copy(g + QSLOTS).start()
-        else:
-            j = g + QSLOTS - GROUPS
-            k_copy(j).start()
-            v_copy(j).start()
-            if j < WSLOTS:
-                w_copy(wu_hbm, j, j).start()
+        y = lax.dot_general(wqbuf[g * QROWS:(g + 1) * QROWS, :], ain[...], (((1,), (1,)), ((), ())), preferred_element_type=f32)
         y = y.astype(bf16).astype(f32)
         feat = slice(g * HEAD, (g + 1) * HEAD)
         q_sc[feat, :] = rotate(y[:HEAD]).astype(bf16).astype(f32)
         kt_sc[feat, :] = rotate(y[HEAD:2 * HEAD]).astype(bf16).astype(f32)
         vt_sc[feat, :] = y[2 * HEAD:]
-    pltpu.make_async_copy(wo_hbm, wobuf, wosem).start()
+    wo_copy().start()
     qrows = ctx
     for c in range(KV // 128):
         qrows[:, c * 128:(c + 1) * 128] = q_sc[c * 128:(c + 1) * 128, :].T
@@ -124,8 +126,6 @@
             hit = c_lane == t
             kbuf[b] = jnp.where(hit, pltpu.roll(kt_sc[...], shift, 1).astype(bf16), kbuf[b])
             vbuf[b] = jnp.where(hit, pltpu.roll(vt_sc[...], shift, 1).astype(bf16), vbuf[b])
-        ko_copy(i).start()
-        vo_copy(i).start()
         picked = []
         for j in range(0, BLK, 2):
             b0, b1 = base + j, base + j + 1
@@ -153,8 +153,7 @@
 
         @pl.when(i + 4 < NBLK)
         def _():
-            k_copy(i + 4).start()
-            v_copy(i + 4).start()
+            kv_start(i + 4)
 
     def up_body(c, _):
         w_copy(wu_hbm, c, c).wait()
@@ -193,51 +192,61 @@
     lax.fori_loop(0, NW, down_body, 0)
     lax.fori_loop(2 * NW, NBLK, rest_body, 0)
 
-    pltpu.make_async_copy(wo_hbm, wobuf, wosem).wait()
-    cb = ctx[...].astype(bf16)
+    wo_copy().wait()
+    core = lax.rem(lax.axis_index('tp'), 2)
+    mine_rows = pl.ds(pl.multiple_of(core * HALF_ROWS, HALF_ROWS), HALF_ROWS)
+    near_rows = pl.ds(pl.multiple_of((1 - core) * HALF_ROWS, HALF_ROWS), HALF_ROWS)
 
     def out_body(c, _):
         cols = pl.ds(pl.multiple_of(c * WCOLS, WCOLS), WCOLS)
-        part_ref[:, cols] = (acc[:, cols] + jnp.dot(cb, wobuf[:, cols], preferred_element_type=f32)).astype(bf16)
+        w = wqbuf[0:KV, cols]
+        send_ref[:, cols] = (acc[near_rows, cols] + jnp.dot(ctx[near_rows, :].astype(bf16), w, preferred_element_type=f32)).astype(bf16)
+        keep_ref[:, cols] = acc[mine_rows, cols] + jnp.dot(ctx[mine_rows, :].astype(bf16), w, preferred_element_type=f32)
         return 0
 
     lax.fori_loop(0, NW, out_body, 0)
-
-    def drain(i, _):
-        ko_copy(i).wait()
-        vo_copy(i).wait()
-        return 0
-
-    lax.fori_loop(0, NBLK, drain, 0)
-
-
-def reduce_kernel(part, x_ref, out_ref, near, far, mine, fin, peer_half,
-                  s1, r1, s2, r2, s3, r3):
-    f32, bf16 = jnp.float32, jnp.bfloat16
-    me = lax.axis_index('tp')
-    core = lax.rem(me, 2)
-    near_id = me + 1 - 2 * core
-    far_id = lax.rem(me + 2, 4)
-    half = ROWS // 2
-    barrier = pltpu.get_barrier_semaphore()
-    for peer in (near_id, far_id):
-        pl.semaphore_signal(barrier, inc=1, device_id={'tp': peer}, device_id_type=MESH)
-    pl.semaphore_wait(barrier, 2)
-    mine_rows = pl.ds(pl.multiple_of(core * half, half), half)
-    near_rows = pl.ds(pl.multiple_of((1 - core) * half, half), half)
-    c1 = pltpu.make_async_remote_copy(part.at[near_rows], near, s1, r1, device_id={'tp': near_id}, device_id_type=MESH)
-    c1.start()
-    c1.wait()
-    mine[...] = (part[mine_rows, :].astype(f32) + near[...].astype(f32)).astype(bf16)
-    c2 = pltpu.make_async_remote_copy(mine, far, s2, r2, device_id={'tp': far_id}, device_id_type=MESH)
-    c2.start()
-    c2.wait()
-    fin[...] = (mine[...].astype(f32) + far[...].astype(f32) + x_ref[mine_rows, :].astype(f32)).astype(bf16)
-    c3 = pltpu.make_async_remote_copy(fin, peer_half, s3, r3, device_id={'tp': near_id}, device_id_type=MESH)
-    c3.start()
-    out_ref[mine_rows, :] = fin[...]
-    c3.wait()
-    out_ref[near_rows, :] = peer_half[...]
+    xh_ref[...] = x_ref[mine_rows, :]
+
+
+def add_near(keep, near, mine):
+    mine[...] = (keep[...] + near[...].astype(jnp.float32)).astype(jnp.bfloat16)
+
+
+def add_far(mine, far, xh, fin):
+    f32 = jnp.float32
+    fin[...] = (mine[...].astype(f32) + far[...].astype(f32) + xh[...].astype(f32)).astype(jnp.bfloat16)
+
+
+def assemble(fin, other, out_hbm, sem):
+    core = lax.rem(lax.axis_index('tp'), 2)
+    copies = []
+    for n, (src, place) in enumerate(((fin, core), (other, 1 - core))):
+        rows = pl.ds(pl.multiple_of(place * HALF_ROWS, HALF_ROWS), HALF_ROWS)
+        copies.append(pltpu.make_async_copy(src, out_hbm.at[rows], sem.at[n]))
+    for c in copies:
+        c.start()
+    for c in copies:
+        c.wait()
+
+
+def write_rows(first, last, kbuf, vbuf, ko_hbm, vo_hbm, sem):
+    copies = []
+    for n, (src, dst) in enumerate(((kbuf, ko_hbm), (vbuf, vo_hbm))):
+        for r in range(first, last, BLK):
+            rows = pl.ds(r, BLK)
+            copies.append(pltpu.make_async_copy(src.at[rows], dst.at[rows], sem.at[n]))
+    for c in copies:
+        c.start()
+    for c in copies:
+        c.wait()
+
+
+def first_writer(first, last, kbuf, vbuf, ko_hbm, vo_hbm, kout, vout, sem):
+    write_rows(first, last, kbuf, vbuf, ko_hbm, vo_hbm, sem)
+
+
+def next_writer(first, last, kbuf, vbuf, ko_in, vo_in, ko_hbm, vo_hbm, kout, vout, sem):
+    write_rows(first, last, kbuf, vbuf, ko_hbm, vo_hbm, sem)
 
 
 def solution(mesh):
@@ -253,42 +262,72 @@
     sspec = pl.BlockSpec(memory_space=pltpu.SMEM)
     dma = pltpu.SemaphoreType.DMA
 
+    cache = (ROWS, KV, SEQ)
     main = pl.pallas_call(
         main_kernel,
-        out_shape=(sds((ROWS, D), bf16), sds((ROWS, KV, SEQ), bf16), sds((ROWS, KV, SEQ), bf16)),
-        in_specs=[sspec] + [vspec] * 7 + [anyspec] * 6,
-        out_specs=(vspec, anyspec, anyspec),
+        out_shape=(pltpu.VMEM(cache, bf16), pltpu.VMEM(cache, bf16),
+                   pltpu.VMEM((HALF_ROWS, D), bf16), pltpu.VMEM((HALF_ROWS, D), f32), pltpu.VMEM((HALF_ROWS, D), bf16)),
+        in_specs=[sspec] + [vspec] * 6 + [anyspec] * 7,
+        out_specs=(vspec,) * 5,
         scratch_shapes=[
-            pltpu.VMEM((ROWS, KV, SEQ), bf16), pltpu.VMEM((ROWS, KV, SEQ), bf16),
-            pltpu.VMEM((QSLOTS, 240, D), bf16), pltpu.VMEM((WSLOTS, D, WCOLS), bf16), pltpu.VMEM((KV, D), bf16),
+            pltpu.VMEM((ROWS, D), bf16),
+            pltpu.VMEM((3 * KV, D), bf16), pltpu.VMEM((WSLOTS, D, WCOLS), bf16),
             pltpu.VMEM((ROWS, D), bf16), pltpu.VMEM((ROWS, D), bf16),
             pltpu.VMEM((KV, ROWS), f32), pltpu.VMEM((KV, ROWS), f32), pltpu.VMEM((KV, ROWS), f32),
-            pltpu.VMEM((ROWS, D), bf16), pltpu.VMEM((ROWS, D), f32), pltpu.VMEM((ROWS, KV), f32),
-            dma((NBLK,)), dma((NBLK,)), dma((NBLK,)), dma((NBLK,)), dma((QSLOTS,)), dma((WSLOTS,)), dma,
+            pltpu.VMEM((ROWS, D), f32), pltpu.VMEM((ROWS, KV), f32),
+            dma((NBLK,)), dma((NBLK,)), dma((GROUPS,)), dma((WSLOTS,)), dma, dma,
         ],
-        compiler_params=pltpu.CompilerParams(vmem_limit_bytes=67043328),
+        compiler_params=pltpu.CompilerParams(vmem_limit_bytes=22 << 20),
+        cost_estimate=pl.CostEstimate(flops=5 * 10**9, bytes_accessed=8 * 10**7, transcendentals=0),
         name='layer',
     )
-    half = ROWS // 2
-    reduce = pl.pallas_call(
-        reduce_kernel,
-        out_shape=sds((ROWS, D), bf16),
-        in_specs=[vspec, vspec],
-        out_specs=vspec,
-        scratch_shapes=[pltpu.VMEM((half, D), bf16)] * 5 + [dma] * 6,
-        compiler_params=pltpu.CompilerParams(collective_id=0, has_side_effects=True, vmem_limit_bytes=16 << 20),
-        name='exchange',
-    )
+
+    def writer(first, last, kbuf, vbuf, olds):
+        est = pl.CostEstimate(flops=(last - first) * 10**8, bytes_accessed=(last - first) * 4 * KV * SEQ, transcendentals=0)
+        aliases = {0: 2, 1: 3}
+        if olds:
+            aliases.update({2: 0, 3: 1})
+        return pl.pallas_call(
+            functools.partial(next_writer if olds else first_writer, first, last),
+            out_shape=(sds(cache, bf16), sds(cache, bf16), pltpu.VMEM(cache, bf16), pltpu.VMEM(cache, bf16)),
+            in_specs=[vspec, vspec] + [anyspec] * len(olds),
+            out_specs=(anyspec, anyspec, vspec, vspec),
+            scratch_shapes=[dma((2,))],
+            input_output_aliases=aliases,
+            compiler_params=pltpu.CompilerParams(vmem_limit_bytes=22 << 20),
+            cost_estimate=est,
+            name='write%d' % first,
+        )(kbuf, vbuf, *olds)
+
+    def small(kernel, name):
+        return pl.pallas_call(
+            kernel, out_shape=pltpu.VMEM((HALF_ROWS, D), bf16), out_specs=vspec,
+            compiler_params=pltpu.CompilerParams(vmem_limit_bytes=1 << 20), name=name)
+
+    near_pairs = [(0, 1), (1, 0), (2, 3), (3, 2)]
+    far_pairs = [(0, 2), (2, 0), (1, 3), (3, 1)]
 
     def device_step(x, ga, ba, gm, bm, w_qkv, w_out, w_up, w_down, k_cache, v_cache, positions):
         kt = jnp.swapaxes(k_cache, 2, 3).reshape(ROWS, KV, SEQ)
         vt = jnp.swapaxes(v_cache, 2, 3).reshape(ROWS, KV, SEQ)
         wq = jnp.transpose(w_qkv, (1, 2, 3, 0)).reshape(3 * KV, D)
         wo = w_out.reshape(KV, D)
-        part, ko, vo = main(positions, positions.reshape(1, ROWS), jnp.asarray(inv_tab),
-                            ga.reshape(1, D), ba.reshape(1, D), gm.reshape(1, D), bm.reshape(1, D),
-                            x, wq, wo, w_up, w_down, kt, vt)
-        out = reduce(part, x)
+        kbuf, vbuf, send, keep, xh = main(positions, positions.reshape(1, ROWS), jnp.asarray(inv_tab), ga, ba, gm, bm,
+                                          x, wq, wo, w_up, w_down, kt, vt)
+        near = lax.ppermute(send, 'tp', near_pairs)
+        ko, vo, kbuf, vbuf = writer(0, CUTS[0], kbuf, vbuf, ())
+        mine = small(add_near, 'add_near')(keep, near)
+        mine, ko, vo = lax.optimization_barrier((mine, ko, vo))
+        far = lax.ppermute(mine, 'tp', far_pairs)
+        ko, vo, kbuf, vbuf = writer(CUTS[0], CUTS[1], kbuf, vbuf, (ko, vo))
+        fin = small(add_far, 'add_far')(mine, far, xh)
+        fin, ko, vo = lax.optimization_barrier((fin, ko, vo))
+        other = lax.ppermute(fin, 'tp', near_pairs)
+        ko, vo, kbuf, vbuf = writer(CUTS[1], ROWS, kbuf, vbuf, (ko, vo))
+        out = pl.pallas_call(
+            assemble, out_shape=sds((ROWS, D), bf16), in_specs=[vspec] * 2, out_specs=anyspec,
+            scratch_shapes=[dma((2,))], compiler_params=pltpu.CompilerParams(vmem_limit_bytes=1 << 20), name='assemble',
+        )(fin, other)
         back = lambda c: jnp.swapaxes(c.reshape(ROWS, GROUPS, HEAD, SEQ), 2, 3)
         return out, back(ko), back(vo)
 

time: 73.3 us -> 76.4 us (1.042)
  local copies, waits for them, and re-layouts: 8.25 us -> 0 us
  Pallas kernels: 64 us -> 71.9 us
  starting transfers between devices: 0 us -> 3.57 us
    pallas_call x2 -> x7, Pallas kernels: 64 us -> 71.9 us  [the longest x1 55.8 us: device_step(): main(positions, positions.reshape(1, ROWS), jnp.asarray(inv_tab), ga, ba,...]
    reshape x4 -> x0, local copies, waits for them, and re-layouts: 5.24 us -> none  [the longest x1 1.31 us: device_step(): ga.reshape(1, D)]
    ppermute x0 -> x3, starting transfers between devices: none -> 3.57 us  [the longest x1 2.54 us: device_step(): far = lax.ppermute(mine, 'tp', far_pairs)]
    unnamed x5 -> x0, local copies, waits for them, and re-layouts: 3.01 us -> none
  transfers between devices with their start and end apart: 0 -> 3, of which waited for: 0 -> 0; matrix products, arithmetic and copies ran while one was open for 0% -> 0% of each run, Pallas kernels for 0% -> 20%
where the time goes in v2:
time: 76.4 us; the launch traced here: 76.2 us
  Pallas kernels  71.9 us (94%)
  starting transfers between devices  3.57 us (5%)
    pallas_call x1, Pallas kernels, device_step(): main(positions, positions.reshape(1, ROWS), jnp.asarray(inv_tab), ga, ba,...  55.8 us
    pallas_call x3, Pallas kernels, writer(): pl.pallas_call(functools.partial(next_writer if olds else first_writer, f...  15.1 us
    ppermute x1, starting transfers between devices, device_step(): far = lax.ppermute(mine, 'tp', far_pairs)  2.54 us
  transfers between devices with their start and end apart: 3, of which 0 were waited for; matrix products, arithmetic and copies ran while one was open for 0% of the time, Pallas kernels for 20%

profile of v2, /device:TPU:0, one launch (start us, length us, event | category | flops | bytes accessed | tf_op | source)
XLA Modules:
  0.0 76.2 jit_solution(12220846406372399303)
XLA Ops:
  0.6 55.8 %layer.1 = (bf16[128,640,128]{2,1,0:T(8,128)(2,1)S(1)}, bf16[128,640,128]{2,1,0:T(8,128)(2,1)S(1)}, bf16[64,2560]{1,0:T(8,128)(2,1)S(1)}, f32[64,2560]{1,0:T(8,128)S(1)}, bf16[64,2560]{1,0:T(8,128)(2,1)S(1)}) custom-call(s32[128]{0:T(128)} %pos_smem.1, s32[1,128]{1,0:T(1,128)} %bitcast.23, f32[40,128]{1,0:T(8,128)} %constant.2.clone.inv_freq, f32[2560]{0:T(1024)} %ga.1, ...), custom_call_target="tpu_custom_call" | custom-call | flops 5000000000 | bytes 80000000 | tf_op jit(solution)/shard_map/layer/pallas_call | solution.py:315
  56.4 0.8 %collective-permute-start = (bf16[64,2560]{1,0:T(8,128)(2,1)S(1)}, bf16[64,2560]{1,0:T(8,128)(2,1)S(1)}, u32[]{:S(2)}, u32[]{:S(2)}) collective-permute-start(bf16[64,2560]{1,0:T(8,128)(2,1)S(1)} %get-tuple-element.25), channel_id=1, source_target_pairs={{0,1},{1,0},{2,3},{3,2},{4,5},{5,4},{6,7},{7,6},{8,9},{9,8},{10,11... | collective-permute-start | bytes 983048 | tf_op jit(solution)/shard_map/ppermute | solution.py:317
  57.2 3.2 %write0.1 = (bf16[128,640,128]{2,1,0:T(8,128)(2,1)}, bf16[128,640,128]{2,1,0:T(8,128)(2,1)}, bf16[128,640,128]{2,1,0:T(8,128)(2,1)S(1)}, bf16[128,640,128]{2,1,0:T(8,128)(2,1)S(1)}) custom-call(bf16[128,640,128]{2,1,0:T(8,128)(2,1)S(1)} %get-tuple-element.26.kbuf, ...), custom_call_target="tpu_custom_call", output_to_operand_aliasing={{2}: (0, {}), {3}: (1, {})} | custom-call | flops 2400000000 | bytes 7864320 | tf_op jit(solution)/shard_map/write0/pallas_call | solution.py:290
  60.4 0.0 collective-permute-done.near
  60.4 0.1 add_near.1.mine
  60.5 2.5 %collective-permute-start.1 = (bf16[64,2560]{1,0:T(8,128)(2,1)S(1)}, bf16[64,2560]{1,0:T(8,128)(2,1)S(1)}, u32[]{:S(2)}, u32[]{:S(2)}) collective-permute-start(bf16[64,2560]{1,0:T(8,128)(2,1)S(1)} %add_near.1.mine), channel_id=1, source_target_pairs={{0,2},{2,0},{1,3},{3,1},{4,6},{6,4},{5,7},{7,5},{8,10},{10,8},{9,1... | collective-permute-start | bytes 983048 | tf_op jit(solution)/shard_map/ppermute | solution.py:321
  63.0 8.7 %write24.1 = (bf16[128,640,128]{2,1,0:T(8,128)(2,1)}, bf16[128,640,128]{2,1,0:T(8,128)(2,1)}, bf16[128,640,128]{2,1,0:T(8,128)(2,1)S(1)}, bf16[128,640,128]{2,1,0:T(8,128)(2,1)S(1)}) custom-call(bf16[128,640,128]{2,1,0:T(8,128)(2,1)S(1)} %get-tuple-element.32.kbuf, ...), custom_call_target="tpu_custom_call", output_to_operand_aliasing={{2}: (0, {}), {3}: (1, {}), {0}: (2, {}), {1}: (3, {})} | custom-call | flops 8000000000 | bytes 26214400 | tf_op jit(solution)/shard_map/write24/pallas_call | solution.py:290
  71.7 0.0 collective-permute-done.1.far
  71.7 0.1 add_far.1.fin
  71.9 0.2 collective-permute-start.2
  72.1 3.2 %write104.1 = (bf16[128,640,128]{2,1,0:T(8,128)(2,1)}, bf16[128,640,128]{2,1,0:T(8,128)(2,1)}, bf16[128,640,128]{2,1,0:T(8,128)(2,1)S(1)}, bf16[128,640,128]{2,1,0:T(8,128)(2,1)S(1)}) custom-call(bf16[128,640,128]{2,1,0:T(8,128)(2,1)S(1)} %get-tuple-element.39.kbuf, ...), custom_call_target="tpu_custom_call", output_to_operand_aliasing={{2}: (0, {}), {3}: (1, {}), {0}: (2, {}), {1}: (3, {})} | custom-call | flops 2400000000 | bytes 7864320 | tf_op jit(solution)/shard_map/write104/pallas_call | solution.py:290
  75.3 0.0 collective-permute-done.2.other
  75.3 0.9 %assemble.1 = bf16[128,2560]{1,0:T(8,128)(2,1)} custom-call(bf16[64,2560]{1,0:T(8,128)(2,1)S(1)} %add_far.1.fin, bf16[64,2560]{1,0:T(8,128)(2,1)S(1)} %collective-permute-done.2.other), custom_call_target="tpu_custom_call" | custom-call | tf_op jit(solution)/shard_map/assemble/pallas_call | solution.py:327
Async XLA Ops:
  56.4 4.0 %collective-permute-start = (bf16[64,2560]{1,0:T(8,128)(2,1)S(1)}, bf16[64,2560]{1,0:T(8,128)(2,1)S(1)}, u32[]{:S(2)}, u32[]{:S(2)}) collective-permute-start(bf16[64,2560]{1,0:T(8,128)(2,1)S(1)} %get-tuple-element.25), channel_id=1, source_target_pairs={{0,1},{1,0},{2,3},{3,2},{4,5},{5,4},{6,7},{7,6},{8,9},{9,8},{10,11... | collective-permute-start | bytes 983048 | tf_op jit(solution)/shard_map/ppermute | solution.py:317
  60.5 11.3 %collective-permute-start.1 = (bf16[64,2560]{1,0:T(8,128)(2,1)S(1)}, bf16[64,2560]{1,0:T(8,128)(2,1)S(1)}, u32[]{:S(2)}, u32[]{:S(2)}) collective-permute-start(bf16[64,2560]{1,0:T(8,128)(2,1)S(1)} %add_near.1.mine), channel_id=1, source_target_pairs={{0,2},{2,0},{1,3},{3,1},{4,6},{6,4},{5,7},{7,5},{8,10},{10,8},{9,1... | collective-permute-start | bytes 983048 | tf_op jit(solution)/shard_map/ppermute | solution.py:321
  71.9 3.4 %collective-permute-start.2 = (bf16[64,2560]{1,0:T(8,128)(2,1)S(1)}, bf16[64,2560]{1,0:T(8,128)(2,1)S(1)}, u32[]{:S(2)}, u32[]{:S(2)}) collective-permute-start(bf16[64,2560]{1,0:T(8,128)(2,1)S(1)} %add_far.1.fin), channel_id=1, source_target_pairs={{0,1},{1,0},{2,3},{3,2},{4,5},{5,4},{6,7},{7,6},{8,9},{9,8},{10,11... | collective-permute-start | bytes 983048 | tf_op jit(solution)/shard_map/ppermute | solution.py:325

commit v3 on v2

--- a/solution.py
+++ b/solution.py
@@ -24,36 +24,39 @@
 WCOLS = 512
 NW = D // WCOLS
 WSLOTS = 3
-QROWS = 240
+QROWS = 960
+AHEAD = NBLK - 2 * NW
+OCOLS = 1280
 HALF_ROWS = ROWS // 2
 CUTS = (24, 104)
+LIMIT = 23200 << 10
 
 
 def main_kernel(pos_smem, pos_row, inv_freq, ga, ba, gm, bm, x_hbm, wq_hbm, wo_hbm, wu_hbm, wd_hbm, k_hbm, v_hbm,
                 kbuf, vbuf, send_ref, keep_ref, xh_ref,
-                x_ref, wqbuf, wbuf, ain, min_, q_sc, kt_sc, vt_sc, acc, ctx,
-                ksem, vsem, wqsem, wsem, wosem, xsem):
+                x_ref, wqbuf, wbuf, ain, qrows, kt_sc, vt_sc, acc, ctx, s_sc, p_sc,
+                ksem, vsem, wqsem, wsem, wosem, xsem, xhsem):
     f32, bf16 = jnp.float32, jnp.bfloat16
-    h_sc = ain
-
-    def wq_copy(g):
-        rows = pl.ds(g * QROWS, QROWS)
-        return pltpu.make_async_copy(wq_hbm.at[rows], wqbuf.at[rows], wqsem.at[g])
+    h_sc, min_ = ain, x_ref
+
+    def wq_copy(n):
+        rows = pl.ds(n * QROWS, QROWS)
+        return pltpu.make_async_copy(wq_hbm.at[rows], wqbuf.at[rows], wqsem.at[n])
 
     def wo_copy():
         return pltpu.make_async_copy(wo_hbm, wqbuf.at[pl.ds(0, KV)], wosem)
+
+    def k_copy(i):
+        rows = pl.ds(i * BLK, BLK)
+        return pltpu.make_async_copy(k_hbm.at[rows], kbuf.at[rows], ksem.at[i])
+
+    def v_copy(i):
+        rows = pl.ds(i * BLK, BLK)
+        return pltpu.make_async_copy(v_hbm.at[rows], vbuf.at[rows], vsem.at[i])
 
     def kv_start(i):
         k_copy(i).start()
         v_copy(i).start()
-
-    def k_copy(i):
-        rows = pl.ds(i * BLK, BLK)
-        return pltpu.make_async_copy(k_hbm.at[rows], kbuf.at[rows], ksem.at[i])
-
-    def v_copy(i):
-        rows = pl.ds(i * BLK, BLK)
-        return pltpu.make_async_copy(v_hbm.at[rows], vbuf.at[rows], vsem.at[i])
 
     def w_copy(hbm, c, n):
         cols = pl.ds(pl.multiple_of(c * WCOLS, WCOLS), WCOLS)
@@ -62,18 +65,18 @@
 
     x_copy = pltpu.make_async_copy(x_hbm, x_ref, xsem)
     x_copy.start()
-    for g in range(GROUPS):
-        wq_copy(g).start()
-    for j in range(WSLOTS):
-        kv_start(j)
-        w_copy(wu_hbm, j, j).start()
-    kv_start(WSLOTS)
+    wq_copy(0).start()
     x_copy.wait()
+    wq_copy(1).start()
+    core = lax.rem(lax.axis_index('tp'), 2)
+    mine_rows = pl.ds(pl.multiple_of(core * HALF_ROWS, HALF_ROWS), HALF_ROWS)
+    xh_copy = pltpu.make_async_copy(x_hbm.at[mine_rows], xh_ref, xhsem)
+    xh_copy.start()
+    kv_start(0)
 
     gav, bav, gmv, bmv = [r[...].reshape(1, D) for r in (ga, ba, gm, bm)]
-
-    def ln_body(r, _):
-        rows = pl.ds(pl.multiple_of(r * 16, 16), 16)
+    for r in range(0, ROWS, 16):
+        rows = slice(r, r + 16)
         xf = x_ref[rows, :].astype(f32)
         mean = jnp.mean(xf, axis=-1, keepdims=True)
         cen = xf - mean
@@ -81,9 +84,6 @@
         nrm = cen * lax.rsqrt(var + LN_EPS)
         ain[rows, :] = (nrm * gav + bav).astype(bf16)
         min_[rows, :] = (nrm * gmv + bmv).astype(bf16)
-        return 0
-
-    lax.fori_loop(0, ROWS // 16, ln_body, 0)
 
     angles = inv_freq[...] * pos_row[...].astype(f32)
     cos_t = jnp.cos(angles)
@@ -91,121 +91,146 @@
 
     def rotate(u):
         lo, hi = u[:HALF], u[HALF:]
-        return jnp.concatenate([lo * cos_t - hi * sin_t, hi * cos_t + lo * sin_t], axis=0)
-
-    for g in range(GROUPS):
-        wq_copy(g).wait()
-        y = lax.dot_general(wqbuf[g * QROWS:(g + 1) * QROWS, :], ain[...], (((1,), (1,)), ((), ())), preferred_element_type=f32)
+        return jnp.concatenate([lo * cos_t - hi * sin_t, hi * cos_t + lo * sin_t], axis=0).astype(bf16)
+
+    queries = []
+    for n in range(3 * KV // QROWS):
+        wq_copy(n).wait()
+        w_copy(wu_hbm, n, n).start()
+        kv_start(n + 1)
+        y = lax.dot_general(wqbuf[n * QROWS:(n + 1) * QROWS, :], ain[...], (((1,), (1,)), ((), ())), preferred_element_type=f32)
         y = y.astype(bf16).astype(f32)
-        feat = slice(g * HEAD, (g + 1) * HEAD)
-        q_sc[feat, :] = rotate(y[:HEAD]).astype(bf16).astype(f32)
-        kt_sc[feat, :] = rotate(y[HEAD:2 * HEAD]).astype(bf16).astype(f32)
-        vt_sc[feat, :] = y[2 * HEAD:]
+        for m in range(QROWS // (3 * HEAD)):
+            g = n * (QROWS // (3 * HEAD)) + m
+            yg = y[m * 3 * HEAD:(m + 1) * 3 * HEAD]
+            feat = slice(g * HEAD, (g + 1) * HEAD)
+            queries.append(rotate(yg[:HEAD]).astype(f32))
+            kt_sc[feat, :] = rotate(yg[HEAD:2 * HEAD])
+            vt_sc[feat, :] = yg[2 * HEAD:].astype(bf16)
     wo_copy().start()
-    qrows = ctx
+    w_copy(wu_hbm, 2, 2).start()
+    for i in range(3, AHEAD):
+        kv_start(i)
+    qall = jnp.concatenate(queries, axis=0)
     for c in range(KV // 128):
-        qrows[:, c * 128:(c + 1) * 128] = q_sc[c * 128:(c + 1) * 128, :].T
+        qrows[:, c * 128:(c + 1) * 128] = qall[c * 128:(c + 1) * 128, :].T
 
     lane8 = lax.broadcasted_iota(jnp.int32, (8, KV), 1)
     sub8 = lax.broadcasted_iota(jnp.int32, (8, KV), 0)
     own8 = (lane8 >= sub8 * HEAD) & (lane8 < sub8 * HEAD + HEAD)
     s_lane = lax.broadcasted_iota(jnp.int32, (8, SEQ), 1)
-    c_lane = lax.broadcasted_iota(jnp.int32, (KV, SEQ), 1)
+    c_lane = lax.broadcasted_iota(jnp.int16, (KV, SEQ), 1)
+    top16 = lax.broadcasted_iota(jnp.int32, (16, SEQ), 0) < 8
     sel = (lax.broadcasted_iota(jnp.int32, (BLK, BLK * 8), 1) // 8
            == lax.broadcasted_iota(jnp.int32, (BLK, BLK * 8), 0)).astype(f32).astype(bf16)
-    zero8 = jnp.zeros((8, SEQ), f32)
-
-    def attend(i):
+
+    def arrive(i):
         k_copy(i).wait()
         v_copy(i).wait()
+
+    def scores(i):
         base = pl.multiple_of(i * BLK, BLK)
+        for j in range(0, BLK, 2):
+            qs, ks = [], []
+            for b in (base + j, base + j + 1):
+                t = pos_smem[b]
+                shift = lax.rem(t - b + SEQ, SEQ)
+                hit = c_lane == t.astype(jnp.int16)
+                kn = jnp.where(hit, pltpu.roll(kt_sc[...], shift, 1), kbuf[b])
+                kbuf[b] = kn
+                ks.append(kn)
+                vbuf[b] = jnp.where(hit, pltpu.roll(vt_sc[...], shift, 1), vbuf[b])
+                row = jnp.broadcast_to(qrows[pl.ds(b, 1), :], (8, KV))
+                qs.append(jnp.where(own8, row, 0.0))
+            s2 = jnp.dot(jnp.concatenate(qs, axis=0).astype(bf16), jnp.concatenate(ks, axis=1), preferred_element_type=f32)
+            s_sc[j * 8:j * 8 + 8, :] = s2[:8, :SEQ]
+            s_sc[j * 8 + 8:j * 8 + 16, :] = s2[8:, SEQ:]
+
+    def soften(i):
         for j in range(BLK):
-            b = base + j
-            t = pos_smem[b]
-            shift = lax.rem(t - b + SEQ, SEQ)
-            hit = c_lane == t
-            kbuf[b] = jnp.where(hit, pltpu.roll(kt_sc[...], shift, 1).astype(bf16), kbuf[b])
-            vbuf[b] = jnp.where(hit, pltpu.roll(vt_sc[...], shift, 1).astype(bf16), vbuf[b])
+            s = s_sc[j * 8:j * 8 + 8, :] * (HEAD ** -0.5)
+            s = jnp.where(s_lane <= pos_smem[i * BLK + j], s, NEG_BIG)
+            e = jnp.exp(s - jnp.max(s, axis=-1, keepdims=True))
+            p_sc[j * 8:j * 8 + 8, :] = e / jnp.sum(e, axis=-1, keepdims=True)
+
+    def mix(i):
+        base = pl.multiple_of(i * BLK, BLK)
         picked = []
         for j in range(0, BLK, 2):
-            b0, b1 = base + j, base + j + 1
-            qs = []
-            for b in (b0, b1):
-                row = jnp.broadcast_to(qrows[pl.ds(b, 1), :], (8, KV))
-                qs.append(jnp.where(own8, row, 0.0))
-            qbd = jnp.concatenate(qs, axis=0).astype(bf16)
-            kk = jnp.concatenate([kbuf[b0], kbuf[b1]], axis=1)
-            s2 = jnp.dot(qbd, kk, preferred_element_type=f32)
-            ps = []
-            for n, b in enumerate((b0, b1)):
-                s = s2[n * 8:n * 8 + 8, n * SEQ:(n + 1) * SEQ] * (HEAD ** -0.5)
-                s = jnp.where(s_lane <= pos_smem[b], s, NEG_BIG)
-                e = jnp.exp(s - jnp.max(s, axis=-1, keepdims=True))
-                ps.append(e / jnp.sum(e, axis=-1, keepdims=True))
-            pbd = jnp.concatenate([jnp.concatenate([ps[0], zero8], axis=1),
-                                   jnp.concatenate([zero8, ps[1]], axis=1)], axis=0).astype(bf16)
-            vv = jnp.concatenate([vbuf[b0], vbuf[b1]], axis=1)
+            p = p_sc[j * 8:j * 8 + 16, :]
+            pbd = jnp.concatenate([jnp.where(top16, p, 0.0), jnp.where(top16, 0.0, p)], axis=1).astype(bf16)
+            vv = jnp.concatenate([vbuf[base + j], vbuf[base + j + 1]], axis=1)
             c2 = lax.dot_general(pbd, vv, (((1,), (1,)), ((), ())), preferred_element_type=f32)
             picked.append(jnp.where(own8, c2[:8], 0.0))
             picked.append(jnp.where(own8, c2[8:], 0.0))
         stack = jnp.concatenate(picked, axis=0).astype(bf16)
         ctx[pl.ds(base, BLK), :] = jnp.dot(sel, stack, preferred_element_type=f32)
 
-        @pl.when(i + 4 < NBLK)
-        def _():
-            kv_start(i + 4)
-
-    def up_body(c, _):
-        w_copy(wu_hbm, c, c).wait()
+    def attend(i):
+        mix(jnp.maximum(i - 2, 0))
+        soften(jnp.maximum(i - 1, 0))
+        scores(i)
+
+    def split(y):
+        low, high = y[:HALF_ROWS], y[HALF_ROWS:]
+        return jnp.where(core == 0, low, high), jnp.where(core == 0, high, low)
+
+    def up_dot(c):
         y = jnp.dot(min_[...], wbuf[lax.rem(c, WSLOTS)], preferred_element_type=f32)
         cols = pl.ds(pl.multiple_of(c * WCOLS, WCOLS), WCOLS)
         h_sc[:, cols] = (0.5 * y * (1.0 + lax.erf(y * (0.5 ** 0.5)))).astype(bf16)
-        n = c + WSLOTS
-
-        @pl.when(n < NW)
-        def _():
-            w_copy(wu_hbm, n, n).start()
-
-        @pl.when(n >= NW)
-        def _():
-            w_copy(wd_hbm, n - NW, n).start()
+
+    def down_dot(c, n):
+        cols = pl.ds(pl.multiple_of(c * WCOLS, WCOLS), WCOLS)
+        mine, near = split(jnp.dot(h_sc[...], wbuf[lax.rem(n, WSLOTS)], preferred_element_type=f32))
+        keep_ref[:, cols] = mine
+        acc[:, cols] = near
+
+    s_sc[...] = jnp.zeros_like(s_sc)
+    p_sc[...] = jnp.zeros_like(p_sc)
+
+    def up_body(next_hbm, back, c, _):
+        w_copy(wu_hbm, c, c).wait()
+        arrive(c)
+        up_dot(c)
         attend(c)
+        w_copy(next_hbm, c + WSLOTS - back, c + WSLOTS).start()
+        kv_start(c + AHEAD)
         return 0
 
-    def down_body(c, _):
+    def down_body(more, c, _):
         n = c + NW
         w_copy(wd_hbm, c, n).wait()
-        cols = pl.ds(pl.multiple_of(c * WCOLS, WCOLS), WCOLS)
-        acc[:, cols] = jnp.dot(h_sc[...], wbuf[lax.rem(n, WSLOTS)], preferred_element_type=f32)
-
-        @pl.when(c + WSLOTS < NW)
-        def _():
+        arrive(n)
+        down_dot(c, n)
+        attend(n)
+        if more:
             w_copy(wd_hbm, c + WSLOTS, n + WSLOTS).start()
-        attend(n)
+        kv_start(n + AHEAD)
         return 0
 
     def rest_body(i, _):
+        arrive(i)
         attend(i)
         return 0
 
-    lax.fori_loop(0, NW, up_body, 0)
-    lax.fori_loop(0, NW, down_body, 0)
+    lax.fori_loop(0, NW - WSLOTS, functools.partial(up_body, wu_hbm, 0), 0)
+    lax.fori_loop(NW - WSLOTS, NW, functools.partial(up_body, wd_hbm, NW), 0)
+    lax.fori_loop(0, NW - WSLOTS, functools.partial(down_body, True), 0)
+    lax.fori_loop(NW - WSLOTS, NW, functools.partial(down_body, False), 0)
     lax.fori_loop(2 * NW, NBLK, rest_body, 0)
-
     wo_copy().wait()
-    core = lax.rem(lax.axis_index('tp'), 2)
-    mine_rows = pl.ds(pl.multiple_of(core * HALF_ROWS, HALF_ROWS), HALF_ROWS)
-    near_rows = pl.ds(pl.multiple_of((1 - core) * HALF_ROWS, HALF_ROWS), HALF_ROWS)
-
-    def out_body(c, _):
-        cols = pl.ds(pl.multiple_of(c * WCOLS, WCOLS), WCOLS)
-        w = wqbuf[0:KV, cols]
-        send_ref[:, cols] = (acc[near_rows, cols] + jnp.dot(ctx[near_rows, :].astype(bf16), w, preferred_element_type=f32)).astype(bf16)
-        keep_ref[:, cols] = acc[mine_rows, cols] + jnp.dot(ctx[mine_rows, :].astype(bf16), w, preferred_element_type=f32)
-        return 0
-
-    lax.fori_loop(0, NW, out_body, 0)
-    xh_ref[...] = x_ref[mine_rows, :]
+    mix(NBLK - 2)
+    soften(NBLK - 1)
+    mix(NBLK - 1)
+
+    cb = ctx[...].astype(bf16)
+    for c in range(0, D, OCOLS):
+        cols = slice(c, c + OCOLS)
+        mine, near = split(jnp.dot(cb, wqbuf[0:KV, cols], preferred_element_type=f32))
+        keep_ref[:, cols] += mine
+        send_ref[:, cols] = (acc[:, cols] + near).astype(bf16)
+    xh_copy.wait()
 
 
 def add_near(keep, near, mine):
@@ -272,12 +297,13 @@
         scratch_shapes=[
             pltpu.VMEM((ROWS, D), bf16),
             pltpu.VMEM((3 * KV, D), bf16), pltpu.VMEM((WSLOTS, D, WCOLS), bf16),
-            pltpu.VMEM((ROWS, D), bf16), pltpu.VMEM((ROWS, D), bf16),
-            pltpu.VMEM((KV, ROWS), f32), pltpu.VMEM((KV, ROWS), f32), pltpu.VMEM((KV, ROWS), f32),
-            pltpu.VMEM((ROWS, D), f32), pltpu.VMEM((ROWS, KV), f32),
-            dma((NBLK,)), dma((NBLK,)), dma((GROUPS,)), dma((WSLOTS,)), dma, dma,
+            pltpu.VMEM((ROWS, D), bf16),
+            pltpu.VMEM((ROWS, KV), f32), pltpu.VMEM((KV, ROWS), bf16), pltpu.VMEM((KV, ROWS), bf16),
+            pltpu.VMEM((HALF_ROWS, D), f32), pltpu.VMEM((ROWS, KV), f32),
+            pltpu.VMEM((BLK * 8, SEQ), f32), pltpu.VMEM((BLK * 8, SEQ), f32),
+            dma((NBLK,)), dma((NBLK,)), dma((3 * KV // QROWS,)), dma((WSLOTS,)), dma, dma, dma,
         ],
-        compiler_params=pltpu.CompilerParams(vmem_limit_bytes=22 << 20),
+        compiler_params=pltpu.CompilerParams(vmem_limit_bytes=LIMIT),
         cost_estimate=pl.CostEstimate(flops=5 * 10**9, bytes_accessed=8 * 10**7, transcendentals=0),
         name='layer',
     )
@@ -294,7 +320,7 @@
             out_specs=(anyspec, anyspec, vspec, vspec),
             scratch_shapes=[dma((2,))],
             input_output_aliases=aliases,
-            compiler_params=pltpu.CompilerParams(vmem_limit_bytes=22 << 20),
+            compiler_params=pltpu.CompilerParams(vmem_limit_bytes=LIMIT),
             cost_estimate=est,
             name='write%d' % first,
         )(kbuf, vbuf, *olds)

time: 76.4 us -> 54.1 us (0.71)
  Pallas kernels: 71.9 us -> 47.8 us
  local copies, waits for them, and re-layouts: 0 us -> 1.8 us
    pallas_call x1, Pallas kernels: 55.8 us -> 31.8 us  [device_step(): main(positions, positions.reshape(1, ROWS), jnp.asarray(inv_tab), ga, ba,...]
    unnamed x0 -> x6, local copies, waits for them, and re-layouts: none -> 1.8 us
  transfers between devices with their start and end apart: 3 -> 3, of which waited for: 0 -> 0; matrix products, arithmetic and copies ran while one was open for 0% -> 0% of each run, Pallas kernels for 20% -> 28%
where the time goes in v3:
time: 54.1 us; the launch traced here: 53.9 us
  Pallas kernels  47.8 us (88%)
  starting transfers between devices  3.53 us (7%)
  local copies, waits for them, and re-layouts  1.8 us (3%)
  between operations  0.73 us (1%)
    pallas_call x1, Pallas kernels, device_step(): main(positions, positions.reshape(1, ROWS), jnp.asarray(inv_tab), ga, ba,...  31.8 us
    pallas_call x3, Pallas kernels, writer(): pl.pallas_call(functools.partial(next_writer if olds else first_writer, f...  15 us
    ppermute x1, starting transfers between devices, device_step(): far = lax.ppermute(mine, 'tp', far_pairs)  2.65 us
    unnamed x6, local copies, waits for them, and re-layouts  1.8 us
  transfers between devices with their start and end apart: 3, of which 0 were waited for; matrix products, arithmetic and copies ran while one was open for 0% of the time, Pallas kernels for 28%

profile of v3, /device:TPU:0, one launch (start us, length us, event | category | flops | bytes accessed | tf_op | source)
XLA Modules:
  0.0 53.9 jit_solution(2740507675799907404)
XLA Ops:
  0.6 31.8 %layer.1 = (bf16[128,640,128]{2,1,0:T(8,128)(2,1)S(1)}, bf16[128,640,128]{2,1,0:T(8,128)(2,1)S(1)}, bf16[64,2560]{1,0:T(8,128)(2,1)S(1)}, f32[64,2560]{1,0:T(8,128)S(1)}, bf16[64,2560]{1,0:T(8,128)(2,1)S(1)}) custom-call(s32[128]{0:T(128)} %pos_smem.1, s32[1,128]{1,0:T(1,128)} %bitcast.23, f32[40,128]{1,0:T(8,128)} %constant.2.clone.inv_freq, f32[2560]{0:T(1024)} %ga.1, ...), custom_call_target="tpu_custom_call" | custom-call | flops 5000000000 | bytes 80000000 | tf_op jit(solution)/shard_map/layer/pallas_call | solution.py:341
  32.4 0.0 copy-start.2
  32.4 0.7 %copy-done.2 = bf16[64,2560]{1,0:T(8,128)(2,1)} copy-done((bf16[64,2560]{1,0:T(8,128)(2,1)}, bf16[64,2560]{1,0:T(8,128)(2,1)S(1)}, u32[]{:S(2)}) %copy-start.2) | copy-done | bytes 327704
  33.1 0.0 copy-start
  33.1 0.7 %collective-permute-start = (bf16[64,2560]{1,0:T(8,128)(2,1)}, bf16[64,2560]{1,0:T(8,128)(2,1)S(1)}, u32[]{:S(2)}, u32[]{:S(2)}) collective-permute-start(bf16[64,2560]{1,0:T(8,128)(2,1)} %copy-done.2), channel_id=1, source_target_pairs={{0,1},{1,0},{2,3},{3,2},{4,5},{5,4},{6,7},{7,6},{8,9},{9,8},{10,11... | collective-permute-start | bytes 983048 | tf_op jit(solution)/shard_map/ppermute | solution.py:343
  33.9 3.2 %write0.1 = (bf16[128,640,128]{2,1,0:T(8,128)(2,1)}, bf16[128,640,128]{2,1,0:T(8,128)(2,1)}, bf16[128,640,128]{2,1,0:T(8,128)(2,1)S(1)}, bf16[128,640,128]{2,1,0:T(8,128)(2,1)S(1)}) custom-call(bf16[128,640,128]{2,1,0:T(8,128)(2,1)S(1)} %get-tuple-element.26.kbuf, ...), custom_call_target="tpu_custom_call", output_to_operand_aliasing={{2}: (0, {}), {3}: (1, {})} | custom-call | flops 2400000000 | bytes 7864320 | tf_op jit(solution)/shard_map/write0/pallas_call | solution.py:316
  37.0 0.0 copy-done
  37.0 0.0 collective-permute-done.near
  37.0 0.0 copy-start.1
  37.1 1.1 %copy-done.1 = f32[64,2560]{1,0:T(8,128)S(1)} copy-done((f32[64,2560]{1,0:T(8,128)S(1)}, f32[64,2560]{1,0:T(8,128)}, u32[]{:S(2)}) %copy-start.1) | copy-done | bytes 655384
  38.1 0.1 add_near.1.mine
  38.2 2.6 %collective-permute-start.1 = (bf16[64,2560]{1,0:T(8,128)(2,1)S(1)}, bf16[64,2560]{1,0:T(8,128)(2,1)S(1)}, u32[]{:S(2)}, u32[]{:S(2)}) collective-permute-start(bf16[64,2560]{1,0:T(8,128)(2,1)S(1)} %add_near.1.mine), channel_id=1, source_target_pairs={{0,2},{2,0},{1,3},{3,1},{4,6},{6,4},{5,7},{7,5},{8,10},{10,8},{9,1... | collective-permute-start | bytes 983048 | tf_op jit(solution)/shard_map/ppermute | solution.py:347
  40.8 8.7 %write24.1 = (bf16[128,640,128]{2,1,0:T(8,128)(2,1)}, bf16[128,640,128]{2,1,0:T(8,128)(2,1)}, bf16[128,640,128]{2,1,0:T(8,128)(2,1)S(1)}, bf16[128,640,128]{2,1,0:T(8,128)(2,1)S(1)}) custom-call(bf16[128,640,128]{2,1,0:T(8,128)(2,1)S(1)} %get-tuple-element.32.kbuf, ...), custom_call_target="tpu_custom_call", output_to_operand_aliasing={{2}: (0, {}), {3}: (1, {}), {0}: (2, {}), {1}: (3, {})} | custom-call | flops 8000000000 | bytes 26214400 | tf_op jit(solution)/shard_map/write24/pallas_call | solution.py:316
  49.6 0.0 collective-permute-done.1.far
  49.6 0.1 add_far.1.fin
  49.7 0.1 collective-permute-start.2
  49.8 3.2 %write104.1 = (bf16[128,640,128]{2,1,0:T(8,128)(2,1)}, bf16[128,640,128]{2,1,0:T(8,128)(2,1)}, bf16[128,640,128]{2,1,0:T(8,128)(2,1)S(1)}, bf16[128,640,128]{2,1,0:T(8,128)(2,1)S(1)}) custom-call(bf16[128,640,128]{2,1,0:T(8,128)(2,1)S(1)} %get-tuple-element.39.kbuf, ...), custom_call_target="tpu_custom_call", output_to_operand_aliasing={{2}: (0, {}), {3}: (1, {}), {0}: (2, {}), {1}: (3, {})} | custom-call | flops 2400000000 | bytes 7864320 | tf_op jit(solution)/shard_map/write104/pallas_call | solution.py:316
  53.0 0.0 collective-permute-done.2.other
  53.0 0.9 %assemble.1 = bf16[128,2560]{1,0:T(8,128)(2,1)} custom-call(bf16[64,2560]{1,0:T(8,128)(2,1)S(1)} %add_far.1.fin, bf16[64,2560]{1,0:T(8,128)(2,1)S(1)} %collective-permute-done.2.other), custom_call_target="tpu_custom_call" | custom-call | tf_op jit(solution)/shard_map/assemble/pallas_call | solution.py:353
Async XLA Ops:
  32.4 0.7 %copy-start.2 = (bf16[64,2560]{1,0:T(8,128)(2,1)}, bf16[64,2560]{1,0:T(8,128)(2,1)S(1)}, u32[]{:S(2)}) copy-start(bf16[64,2560]{1,0:T(8,128)(2,1)S(1)} %get-tuple-element.25) | copy-start | bytes 983044
  33.1 3.9 %copy-start = (f32[64,2560]{1,0:T(8,128)}, f32[64,2560]{1,0:T(8,128)S(1)}, u32[]{:S(2)}) copy-start(f32[64,2560]{1,0:T(8,128)S(1)} %get-tuple-element.24.keep) | copy-start | bytes 1966084
  33.1 3.9 %collective-permute-start = (bf16[64,2560]{1,0:T(8,128)(2,1)}, bf16[64,2560]{1,0:T(8,128)(2,1)S(1)}, u32[]{:S(2)}, u32[]{:S(2)}) collective-permute-start(bf16[64,2560]{1,0:T(8,128)(2,1)} %copy-done.2), channel_id=1, source_target_pairs={{0,1},{1,0},{2,3},{3,2},{4,5},{5,4},{6,7},{7,6},{8,9},{9,8},{10,11... | collective-permute-start | bytes 983048 | tf_op jit(solution)/shard_map/ppermute | solution.py:343
  37.0 1.1 %copy-start.1 = (f32[64,2560]{1,0:T(8,128)S(1)}, f32[64,2560]{1,0:T(8,128)}, u32[]{:S(2)}) copy-start(f32[64,2560]{1,0:T(8,128)} %copy-done) | copy-start | bytes 1966084
  38.2 11.4 %collective-permute-start.1 = (bf16[64,2560]{1,0:T(8,128)(2,1)S(1)}, bf16[64,2560]{1,0:T(8,128)(2,1)S(1)}, u32[]{:S(2)}, u32[]{:S(2)}) collective-permute-start(bf16[64,2560]{1,0:T(8,128)(2,1)S(1)} %add_near.1.mine), channel_id=1, source_target_pairs={{0,2},{2,0},{1,3},{3,1},{4,6},{6,4},{5,7},{7,5},{8,10},{10,8},{9,1... | collective-permute-start | bytes 983048 | tf_op jit(solution)/shard_map/ppermute | solution.py:347
  49.7 3.3 %collective-permute-start.2 = (bf16[64,2560]{1,0:T(8,128)(2,1)S(1)}, bf16[64,2560]{1,0:T(8,128)(2,1)S(1)}, u32[]{:S(2)}, u32[]{:S(2)}) collective-permute-start(bf16[64,2560]{1,0:T(8,128)(2,1)S(1)} %add_far.1.fin), channel_id=1, source_target_pairs={{0,1},{1,0},{2,3},{3,2},{4,5},{5,4},{6,7},{7,6},{8,9},{9,8},{10,11... | collective-permute-start | bytes 983048 | tf_op jit(solution)/shard_map/ppermute | solution.py:351

commit v4 on v3

--- a/solution.py
+++ b/solution.py
@@ -28,14 +28,14 @@
 AHEAD = NBLK - 2 * NW
 OCOLS = 1280
 HALF_ROWS = ROWS // 2
-CUTS = (24, 104)
-LIMIT = 23200 << 10
-
-
-def main_kernel(pos_smem, pos_row, inv_freq, ga, ba, gm, bm, x_hbm, wq_hbm, wo_hbm, wu_hbm, wd_hbm, k_hbm, v_hbm,
-                kbuf, vbuf, send_ref, keep_ref, xh_ref,
-                x_ref, wqbuf, wbuf, ain, qrows, kt_sc, vt_sc, acc, ctx, s_sc, p_sc,
-                ksem, vsem, wqsem, wsem, wosem, xsem, xhsem):
+CUTS = (32, 40, 120)
+LIMIT = 22784 << 10
+
+
+def main_kernel(pos_hbm, pos_row_hbm, inv_hbm, ga_hbm, ba_hbm, gm_hbm, bm_hbm, x_hbm, wq_hbm, wo_hbm, wu_hbm, wd_hbm, k_hbm, v_hbm,
+                ko_hbm, vo_hbm, kbuf, vbuf, send_ref, keep_ref, xh_ref,
+                pos_smem, pos_row, inv_freq, ga, ba, gm, bm, x_ref, wqbuf, wbuf, ain, qrows, kt_sc, vt_sc, acc, ctx, s_sc, p_sc,
+                ksem, vsem, wqsem, wsem, wosem, xsem, xhsem, smsem, outsem):
     f32, bf16 = jnp.float32, jnp.bfloat16
     h_sc, min_ = ain, x_ref
 
@@ -64,8 +64,15 @@
         return pltpu.make_async_copy(hbm.at[:, cols], wbuf.at[slot], wsem.at[slot])
 
     x_copy = pltpu.make_async_copy(x_hbm, x_ref, xsem)
+    small = [pltpu.make_async_copy(src, dst, smsem.at[n]) for n, (src, dst) in enumerate((
+        (pos_hbm, pos_smem), (pos_row_hbm, pos_row), (inv_hbm, inv_freq),
+        (ga_hbm, ga), (ba_hbm, ba), (gm_hbm, gm), (bm_hbm, bm)))]
     x_copy.start()
+    for c in small:
+        c.start()
     wq_copy(0).start()
+    for c in small:
+        c.wait()
     x_copy.wait()
     wq_copy(1).start()
     core = lax.rem(lax.axis_index('tp'), 2)
@@ -98,7 +105,9 @@
         wq_copy(n).wait()
         w_copy(wu_hbm, n, n).start()
         kv_start(n + 1)
-        y = lax.dot_general(wqbuf[n * QROWS:(n + 1) * QROWS, :], ain[...], (((1,), (1,)), ((), ())), preferred_element_type=f32)
+        y = jnp.concatenate([
+            lax.dot_general(wqbuf[r:r + QROWS // 2, :], ain[...], (((1,), (1,)), ((), ())), preferred_element_type=f32)
+            for r in (n * QROWS, n * QROWS + QROWS // 2)], axis=0)
         y = y.astype(bf16).astype(f32)
         for m in range(QROWS // (3 * HEAD)):
             g = n * (QROWS // (3 * HEAD)) + m
@@ -218,6 +227,13 @@
     lax.fori_loop(NW - WSLOTS, NW, functools.partial(up_body, wd_hbm, NW), 0)
     lax.fori_loop(0, NW - WSLOTS, functools.partial(down_body, True), 0)
     lax.fori_loop(NW - WSLOTS, NW, functools.partial(down_body, False), 0)
+    outs = []
+    for n, (src, dst) in enumerate(((kbuf, ko_hbm), (vbuf, vo_hbm))):
+        for r in range(0, CUTS[0], BLK):
+            rows = pl.ds(r, BLK)
+            outs.append(pltpu.make_async_copy(src.at[rows], dst.at[rows], outsem.at[n, r // BLK]))
+    for c in outs:
+        c.start()
     lax.fori_loop(2 * NW, NBLK, rest_body, 0)
     wo_copy().wait()
     mix(NBLK - 2)
@@ -231,6 +247,8 @@
         keep_ref[:, cols] += mine
         send_ref[:, cols] = (acc[:, cols] + near).astype(bf16)
     xh_copy.wait()
+    for c in outs:
+        c.wait()
 
 
 def add_near(keep, near, mine):
@@ -266,12 +284,8 @@
         c.wait()
 
 
-def first_writer(first, last, kbuf, vbuf, ko_hbm, vo_hbm, kout, vout, sem):
-    write_rows(first, last, kbuf, vbuf, ko_hbm, vo_hbm, sem)
-
-
-def next_writer(first, last, kbuf, vbuf, ko_in, vo_in, ko_hbm, vo_hbm, kout, vout, sem):
-    write_rows(first, last, kbuf, vbuf, ko_hbm, vo_hbm, sem)
+def writer_kernel(first, last, carried, ko_in, vo_in, *refs):
+    write_rows(first, last, refs[0], refs[1], refs[carried], refs[carried + 1], refs[-1])
 
 
 def solution(mesh):
@@ -290,40 +304,38 @@
     cache = (ROWS, KV, SEQ)
     main = pl.pallas_call(
         main_kernel,
-        out_shape=(pltpu.VMEM(cache, bf16), pltpu.VMEM(cache, bf16),
+        out_shape=(sds(cache, bf16), sds(cache, bf16), pltpu.VMEM(cache, bf16), pltpu.VMEM(cache, bf16),
                    pltpu.VMEM((HALF_ROWS, D), bf16), pltpu.VMEM((HALF_ROWS, D), f32), pltpu.VMEM((HALF_ROWS, D), bf16)),
-        in_specs=[sspec] + [vspec] * 6 + [anyspec] * 7,
-        out_specs=(vspec,) * 5,
+        in_specs=[anyspec] * 14,
+        out_specs=(anyspec,) * 2 + (vspec,) * 5,
         scratch_shapes=[
+            pltpu.SMEM((ROWS,), jnp.int32), pltpu.VMEM((1, ROWS), jnp.int32), pltpu.VMEM((HALF, ROWS), f32),
+            pltpu.VMEM((D,), f32), pltpu.VMEM((D,), f32), pltpu.VMEM((D,), f32), pltpu.VMEM((D,), f32),
             pltpu.VMEM((ROWS, D), bf16),
             pltpu.VMEM((3 * KV, D), bf16), pltpu.VMEM((WSLOTS, D, WCOLS), bf16),
             pltpu.VMEM((ROWS, D), bf16),
             pltpu.VMEM((ROWS, KV), f32), pltpu.VMEM((KV, ROWS), bf16), pltpu.VMEM((KV, ROWS), bf16),
             pltpu.VMEM((HALF_ROWS, D), f32), pltpu.VMEM((ROWS, KV), f32),
             pltpu.VMEM((BLK * 8, SEQ), f32), pltpu.VMEM((BLK * 8, SEQ), f32),
-            dma((NBLK,)), dma((NBLK,)), dma((3 * KV // QROWS,)), dma((WSLOTS,)), dma, dma, dma,
+            dma((NBLK,)), dma((NBLK,)), dma((3 * KV // QROWS,)), dma((WSLOTS,)), dma, dma, dma, dma((7,)), dma((2, CUTS[0] // BLK)),
         ],
         compiler_params=pltpu.CompilerParams(vmem_limit_bytes=LIMIT),
         cost_estimate=pl.CostEstimate(flops=5 * 10**9, bytes_accessed=8 * 10**7, transcendentals=0),
         name='layer',
     )
 
-    def writer(first, last, kbuf, vbuf, olds):
-        est = pl.CostEstimate(flops=(last - first) * 10**8, bytes_accessed=(last - first) * 4 * KV * SEQ, transcendentals=0)
-        aliases = {0: 2, 1: 3}
-        if olds:
-            aliases.update({2: 0, 3: 1})
+    def writer(first, last, ko, vo, *carry):
         return pl.pallas_call(
-            functools.partial(next_writer if olds else first_writer, first, last),
-            out_shape=(sds(cache, bf16), sds(cache, bf16), pltpu.VMEM(cache, bf16), pltpu.VMEM(cache, bf16)),
-            in_specs=[vspec, vspec] + [anyspec] * len(olds),
-            out_specs=(anyspec, anyspec, vspec, vspec),
+            functools.partial(writer_kernel, first, last, len(carry)),
+            out_shape=(sds(cache, bf16), sds(cache, bf16)) + tuple(pltpu.VMEM(c.shape, c.dtype) for c in carry),
+            in_specs=[anyspec, anyspec] + [vspec] * len(carry),
+            out_specs=(anyspec, anyspec) + (vspec,) * len(carry),
             scratch_shapes=[dma((2,))],
-            input_output_aliases=aliases,
+            input_output_aliases={n: n for n in range(2 + len(carry))},
             compiler_params=pltpu.CompilerParams(vmem_limit_bytes=LIMIT),
-            cost_estimate=est,
+            cost_estimate=pl.CostEstimate(flops=(last - first) * 10**8, bytes_accessed=(last - first) * 4 * KV * SEQ, transcendentals=0),
             name='write%d' % first,
-        )(kbuf, vbuf, *olds)
+        )(ko, vo, *carry)
 
     def small(kernel, name):
         return pl.pallas_call(
@@ -338,18 +350,18 @@
         vt = jnp.swapaxes(v_cache, 2, 3).reshape(ROWS, KV, SEQ)
         wq = jnp.transpose(w_qkv, (1, 2, 3, 0)).reshape(3 * KV, D)
         wo = w_out.reshape(KV, D)
-        kbuf, vbuf, send, keep, xh = main(positions, positions.reshape(1, ROWS), jnp.asarray(inv_tab), ga, ba, gm, bm,
+        ko, vo, kbuf, vbuf, send, keep, xh = main(positions, positions.reshape(1, ROWS), jnp.asarray(inv_tab), ga, ba, gm, bm,
                                           x, wq, wo, w_up, w_down, kt, vt)
         near = lax.ppermute(send, 'tp', near_pairs)
-        ko, vo, kbuf, vbuf = writer(0, CUTS[0], kbuf, vbuf, ())
+        ko, vo, kbuf, vbuf, keep, xh = writer(CUTS[0], CUTS[1], ko, vo, kbuf, vbuf, keep, xh)
         mine = small(add_near, 'add_near')(keep, near)
         mine, ko, vo = lax.optimization_barrier((mine, ko, vo))
         far = lax.ppermute(mine, 'tp', far_pairs)
-        ko, vo, kbuf, vbuf = writer(CUTS[0], CUTS[1], kbuf, vbuf, (ko, vo))
+        ko, vo, kbuf, vbuf, xh = writer(CUTS[1], CUTS[2], ko, vo, kbuf, vbuf, xh)
         fin = small(add_far, 'add_far')(mine, far, xh)
         fin, ko, vo = lax.optimization_barrier((fin, ko, vo))
         other = lax.ppermute(fin, 'tp', near_pairs)
-        ko, vo, kbuf, vbuf = writer(CUTS[1], ROWS, kbuf, vbuf, (ko, vo))
+        ko, vo, kbuf, vbuf = writer(CUTS[2], ROWS, ko, vo, kbuf, vbuf)
         out = pl.pallas_call(
             assemble, out_shape=sds((ROWS, D), bf16), in_specs=[vspec] * 2, out_specs=anyspec,
             scratch_shapes=[dma((2,))], compiler_params=pltpu.CompilerParams(vmem_limit_bytes=1 << 20), name='assemble',

time: 54.1 us -> 49.4 us (0.913)
  Pallas kernels: 47.8 us -> 44.9 us
  local copies, waits for them, and re-layouts: 1.8 us -> 0 us
    pallas_call x3, Pallas kernels: 15 us -> 11.7 us  [writer(): pl.pallas_call(functools.partial(writer_kernel, first, last, len(carry)),...]
    unnamed x6 -> x0, local copies, waits for them, and re-layouts: 1.8 us -> none
  transfers between devices with their start and end apart: 3 -> 3, of which waited for: 0 -> 0; matrix products, arithmetic and copies ran while one was open for 0% -> 0% of each run, Pallas kernels for 28% -> 24%
where the time goes in v4:
time: 49.4 us; the launch traced here: 49.2 us
  Pallas kernels  44.9 us (91%)
  starting transfers between devices  3.57 us (7%)
  between operations  0.71 us (1%)
    pallas_call x1, Pallas kernels, device_step(): main(positions, positions.reshape(1, ROWS), jnp.asarray(inv_tab), ga, ba,...  32.2 us
    pallas_call x3, Pallas kernels, writer(): pl.pallas_call(functools.partial(writer_kernel, first, last, len(carry)),...  11.7 us
    ppermute x1, starting transfers between devices, device_step(): far = lax.ppermute(mine, 'tp', far_pairs)  2.62 us
  transfers between devices with their start and end apart: 3, of which 0 were waited for; matrix products, arithmetic and copies ran while one was open for 0% of the time, Pallas kernels for 24%

profile of v4, /device:TPU:0, one launch (start us, length us, event | category | flops | bytes accessed | tf_op | source)
XLA Modules:
  0.0 49.2 jit_solution(16176002335588891342)
XLA Ops:
  0.6 32.2 %layer.1 = (bf16[128,640,128]{2,1,0:T(8,128)(2,1)}, bf16[128,640,128]{2,1,0:T(8,128)(2,1)}, bf16[128,640,128]{2,1,0:T(8,128)(2,1)S(1)}, bf16[128,640,128]{2,1,0:...) custom-call(s32[128]{0:T(128)} %pos_hbm.1, ...), custom_call_target="tpu_custom_call" | custom-call | flops 5000000000 | bytes 80000000 | tf_op jit(solution)/shard_map/layer/pallas_call | solution.py:353
  32.8 0.8 %collective-permute-start = (bf16[64,2560]{1,0:T(8,128)(2,1)S(1)}, bf16[64,2560]{1,0:T(8,128)(2,1)S(1)}, u32[]{:S(2)}, u32[]{:S(2)}) collective-permute-start(bf16[64,2560]{1,0:T(8,128)(2,1)S(1)} %get-tuple-element.36), channel_id=1, source_target_pairs={{0,1},{1,0},{2,3},{3,2},{4,5},{5,4},{6,7},{7,6},{8,9},{9,8},{10,11... | collective-permute-start | bytes 983048 | tf_op jit(solution)/shard_map/ppermute | solution.py:355
  33.6 1.5 %write32.1 = (bf16[128,640,128]{2,1,0:T(8,128)(2,1)}, bf16[128,640,128]{2,1,0:T(8,128)(2,1)}, bf16[128,640,128]{2,1,0:T(8,128)(2,1)S(1)}, bf16[128,640,128]{2,1,...) custom-call(bf16[128,640,128]{2,1,0:T(8,128)(2,1)} %get-tuple-elemen, ...), custom_call_target="tpu_custom_call", output_to_operand_aliasing={{0}: (0, {}), {1}: (1, {}), {2}: (2, {}), {3}: (3, {}), {4}... | custom-call | flops 800000000 | bytes 2621440 | tf_op jit(solution)/shard_map/write32/pallas_call | solution.py:328
  35.1 0.0 collective-permute-done.near
  35.1 0.1 add_near.1.mine
  35.2 2.6 %collective-permute-start.1 = (bf16[64,2560]{1,0:T(8,128)(2,1)S(1)}, bf16[64,2560]{1,0:T(8,128)(2,1)S(1)}, u32[]{:S(2)}, u32[]{:S(2)}) collective-permute-start(bf16[64,2560]{1,0:T(8,128)(2,1)S(1)} %add_near.1.mine), channel_id=1, source_target_pairs={{0,2},{2,0},{1,3},{3,1},{4,6},{6,4},{5,7},{7,5},{8,10},{10,8},{9,1... | collective-permute-start | bytes 983048 | tf_op jit(solution)/shard_map/ppermute | solution.py:359
  37.8 8.7 %write40.1 = (bf16[128,640,128]{2,1,0:T(8,128)(2,1)}, bf16[128,640,128]{2,1,0:T(8,128)(2,1)}, bf16[128,640,128]{2,1,0:T(8,128)(2,1)S(1)}, bf16[128,640,128]{2,1,0:T(8,128)(2,1)S(1)}, bf16[64,2560]{1,0:T(8,128)(2,1)S(1)}) custom-call(bf16[128,640,128]{2,1,0:T(8,128)(2,1)} %get-tuple-elemen, ...), custom_call_target="tpu_custom_call", output_to_operand_aliasing={{0}: (0, {}), {1}: (1, {}), {2}: (2, {}), {3}: (3, {}), {4}... | custom-call | flops 8000000000 | bytes 26214400 | tf_op jit(solution)/shard_map/write40/pallas_call | solution.py:328
  46.5 0.0 collective-permute-done.1.far
  46.5 0.1 add_far.1.fin
  46.7 0.2 collective-permute-start.2
  46.8 1.5 %write120.1 = (bf16[128,640,128]{2,1,0:T(8,128)(2,1)}, bf16[128,640,128]{2,1,0:T(8,128)(2,1)}, bf16[128,640,128]{2,1,0:T(8,128)(2,1)S(1)}, bf16[128,640,128]{2,1,0:T(8,128)(2,1)S(1)}) custom-call(bf16[128,640,128]{2,1,0:T(8,128)(2,1)} %get-tuple-element.49.ko_in, ...), custom_call_target="tpu_custom_call", output_to_operand_aliasing={{0}: (0, {}), {1}: (1, {}), {2}: (2, {}), {3}: (3, {})} | custom-call | flops 800000000 | bytes 2621440 | tf_op jit(solution)/shard_map/write120/pallas_call | solution.py:328
  48.4 0.0 collective-permute-done.2.other
  48.4 0.9 %assemble.1 = bf16[128,2560]{1,0:T(8,128)(2,1)} custom-call(bf16[64,2560]{1,0:T(8,128)(2,1)S(1)} %add_far.1.fin, bf16[64,2560]{1,0:T(8,128)(2,1)S(1)} %collective-permute-done.2.other), custom_call_target="tpu_custom_call" | custom-call | tf_op jit(solution)/shard_map/assemble/pallas_call | solution.py:365
Async XLA Ops:
  32.8 2.3 %collective-permute-start = (bf16[64,2560]{1,0:T(8,128)(2,1)S(1)}, bf16[64,2560]{1,0:T(8,128)(2,1)S(1)}, u32[]{:S(2)}, u32[]{:S(2)}) collective-permute-start(bf16[64,2560]{1,0:T(8,128)(2,1)S(1)} %get-tuple-element.36), channel_id=1, source_target_pairs={{0,1},{1,0},{2,3},{3,2},{4,5},{5,4},{6,7},{7,6},{8,9},{9,8},{10,11... | collective-permute-start | bytes 983048 | tf_op jit(solution)/shard_map/ppermute | solution.py:355
  35.2 11.3 %collective-permute-start.1 = (bf16[64,2560]{1,0:T(8,128)(2,1)S(1)}, bf16[64,2560]{1,0:T(8,128)(2,1)S(1)}, u32[]{:S(2)}, u32[]{:S(2)}) collective-permute-start(bf16[64,2560]{1,0:T(8,128)(2,1)S(1)} %add_near.1.mine), channel_id=1, source_target_pairs={{0,2},{2,0},{1,3},{3,1},{4,6},{6,4},{5,7},{7,5},{8,10},{10,8},{9,1... | collective-permute-start | bytes 983048 | tf_op jit(solution)/shard_map/ppermute | solution.py:359
  46.7 1.7 %collective-permute-start.2 = (bf16[64,2560]{1,0:T(8,128)(2,1)S(1)}, bf16[64,2560]{1,0:T(8,128)(2,1)S(1)}, u32[]{:S(2)}, u32[]{:S(2)}) collective-permute-start(bf16[64,2560]{1,0:T(8,128)(2,1)S(1)} %add_far.1.fin), channel_id=1, source_target_pairs={{0,1},{1,0},{2,3},{3,2},{4,5},{5,4},{6,7},{7,6},{8,9},{9,8},{10,11... | collective-permute-start | bytes 983048 | tf_op jit(solution)/shard_map/ppermute | solution.py:363

commit v5 on v4

--- a/solution.py
+++ b/solution.py
@@ -25,7 +25,7 @@
 NW = D // WCOLS
 WSLOTS = 3
 QROWS = 960
-AHEAD = NBLK - 2 * NW
+AHEAD = 3
 OCOLS = 1280
 HALF_ROWS = ROWS // 2
 CUTS = (32, 40, 120)
@@ -79,7 +79,6 @@
     mine_rows = pl.ds(pl.multiple_of(core * HALF_ROWS, HALF_ROWS), HALF_ROWS)
     xh_copy = pltpu.make_async_copy(x_hbm.at[mine_rows], xh_ref, xhsem)
     xh_copy.start()
-    kv_start(0)
 
     gav, bav, gmv, bmv = [r[...].reshape(1, D) for r in (ga, ba, gm, bm)]
     for r in range(0, ROWS, 16):
@@ -103,8 +102,14 @@
     queries = []
     for n in range(3 * KV // QROWS):
         wq_copy(n).wait()
-        w_copy(wu_hbm, n, n).start()
-        kv_start(n + 1)
+        if n == 0:
+            kv_start(0)
+            w_copy(wu_hbm, 0, 0).start()
+            kv_start(1)
+        else:
+            w_copy(wu_hbm, 1, 1).start()
+            kv_start(2)
+            w_copy(wu_hbm, 2, 2).start()
         y = jnp.concatenate([
             lax.dot_general(wqbuf[r:r + QROWS // 2, :], ain[...], (((1,), (1,)), ((), ())), preferred_element_type=f32)
             for r in (n * QROWS, n * QROWS + QROWS // 2)], axis=0)
@@ -116,8 +121,6 @@
             queries.append(rotate(yg[:HEAD]).astype(f32))
             kt_sc[feat, :] = rotate(yg[HEAD:2 * HEAD])
             vt_sc[feat, :] = yg[2 * HEAD:].astype(bf16)
-    wo_copy().start()
-    w_copy(wu_hbm, 2, 2).start()
     for i in range(3, AHEAD):
         kv_start(i)
     qall = jnp.concatenate(queries, axis=0)
@@ -218,15 +221,18 @@
         kv_start(n + AHEAD)
         return 0
 
-    def rest_body(i, _):
+    def rest_body(more, i, _):
         arrive(i)
         attend(i)
+        if more:
+            kv_start(i + AHEAD)
         return 0
 
     lax.fori_loop(0, NW - WSLOTS, functools.partial(up_body, wu_hbm, 0), 0)
     lax.fori_loop(NW - WSLOTS, NW, functools.partial(up_body, wd_hbm, NW), 0)
     lax.fori_loop(0, NW - WSLOTS, functools.partial(down_body, True), 0)
     lax.fori_loop(NW - WSLOTS, NW, functools.partial(down_body, False), 0)
+    wo_copy().start()
     outs = []
     for n, (src, dst) in enumerate(((kbuf, ko_hbm), (vbuf, vo_hbm))):
         for r in range(0, CUTS[0], BLK):
@@ -234,7 +240,8 @@
             outs.append(pltpu.make_async_copy(src.at[rows], dst.at[rows], outsem.at[n, r // BLK]))
     for c in outs:
         c.start()
-    lax.fori_loop(2 * NW, NBLK, rest_body, 0)
+    lax.fori_loop(2 * NW, NBLK - AHEAD, functools.partial(rest_body, True), 0)
+    lax.fori_loop(NBLK - AHEAD, NBLK, functools.partial(rest_body, False), 0)
     wo_copy().wait()
     mix(NBLK - 2)
     soften(NBLK - 1)

time: 49.4 us -> 51 us (1.032)
  Pallas kernels: 44.9 us -> 46.6 us
    pallas_call x1, Pallas kernels: 32.2 us -> 33.8 us  [device_step(): main(positions, positions.reshape(1, ROWS), jnp.asarray(inv_tab), ga, ba,...]
  transfers between devices with their start and end apart: 3 -> 3, of which waited for: 0 -> 0; matrix products, arithmetic and copies ran while one was open for 0% -> 0% of each run, Pallas kernels for 24% -> 23%
where the time goes in v5:
time: 51 us; the launch traced here: 50.8 us
  Pallas kernels  46.6 us (91%)
  starting transfers between devices  3.57 us (7%)
  between operations  0.71 us (1%)
    pallas_call x1, Pallas kernels, device_step(): main(positions, positions.reshape(1, ROWS), jnp.asarray(inv_tab), ga, ba,...  33.8 us
    pallas_call x3, Pallas kernels, writer(): pl.pallas_call(functools.partial(writer_kernel, first, last, len(carry)),...  11.7 us
    ppermute x1, starting transfers between devices, device_step(): far = lax.ppermute(mine, 'tp', far_pairs)  2.63 us
  transfers between devices with their start and end apart: 3, of which 0 were waited for; matrix products, arithmetic and copies ran while one was open for 0% of the time, Pallas kernels for 23%

profile of v5, /device:TPU:0, one launch (start us, length us, event | category | flops | bytes accessed | tf_op | source)
XLA Modules:
  0.0 50.8 jit_solution(9157779469913693499)
XLA Ops:
  0.6 33.8 %layer.1 = (bf16[128,640,128]{2,1,0:T(8,128)(2,1)}, bf16[128,640,128]{2,1,0:T(8,128)(2,1)}, bf16[128,640,128]{2,1,0:T(8,128)(2,1)S(1)}, bf16[128,640,128]{2,1,0:...) custom-call(s32[128]{0:T(128)} %pos_hbm.1, ...), custom_call_target="tpu_custom_call" | custom-call | flops 5000000000 | bytes 80000000 | tf_op jit(solution)/shard_map/layer/pallas_call | solution.py:360
  34.5 0.8 %collective-permute-start = (bf16[64,2560]{1,0:T(8,128)(2,1)S(1)}, bf16[64,2560]{1,0:T(8,128)(2,1)S(1)}, u32[]{:S(2)}, u32[]{:S(2)}) collective-permute-start(bf16[64,2560]{1,0:T(8,128)(2,1)S(1)} %get-tuple-element.36), channel_id=1, source_target_pairs={{0,1},{1,0},{2,3},{3,2},{4,5},{5,4},{6,7},{7,6},{8,9},{9,8},{10,11... | collective-permute-start | bytes 983048 | tf_op jit(solution)/shard_map/ppermute | solution.py:362
  35.2 1.5 %write32.1 = (bf16[128,640,128]{2,1,0:T(8,128)(2,1)}, bf16[128,640,128]{2,1,0:T(8,128)(2,1)}, bf16[128,640,128]{2,1,0:T(8,128)(2,1)S(1)}, bf16[128,640,128]{2,1,...) custom-call(bf16[128,640,128]{2,1,0:T(8,128)(2,1)} %get-tuple-elemen, ...), custom_call_target="tpu_custom_call", output_to_operand_aliasing={{0}: (0, {}), {1}: (1, {}), {2}: (2, {}), {3}: (3, {}), {4}... | custom-call | flops 800000000 | bytes 2621440 | tf_op jit(solution)/shard_map/write32/pallas_call | solution.py:335
  36.7 0.0 collective-permute-done.near
  36.8 0.1 add_near.1.mine
  36.8 2.6 %collective-permute-start.1 = (bf16[64,2560]{1,0:T(8,128)(2,1)S(1)}, bf16[64,2560]{1,0:T(8,128)(2,1)S(1)}, u32[]{:S(2)}, u32[]{:S(2)}) collective-permute-start(bf16[64,2560]{1,0:T(8,128)(2,1)S(1)} %add_near.1.mine), channel_id=1, source_target_pairs={{0,2},{2,0},{1,3},{3,1},{4,6},{6,4},{5,7},{7,5},{8,10},{10,8},{9,1... | collective-permute-start | bytes 983048 | tf_op jit(solution)/shard_map/ppermute | solution.py:366
  39.4 8.7 %write40.1 = (bf16[128,640,128]{2,1,0:T(8,128)(2,1)}, bf16[128,640,128]{2,1,0:T(8,128)(2,1)}, bf16[128,640,128]{2,1,0:T(8,128)(2,1)S(1)}, bf16[128,640,128]{2,1,0:T(8,128)(2,1)S(1)}, bf16[64,2560]{1,0:T(8,128)(2,1)S(1)}) custom-call(bf16[128,640,128]{2,1,0:T(8,128)(2,1)} %get-tuple-elemen, ...), custom_call_target="tpu_custom_call", output_to_operand_aliasing={{0}: (0, {}), {1}: (1, {}), {2}: (2, {}), {3}: (3, {}), {4}... | custom-call | flops 8000000000 | bytes 26214400 | tf_op jit(solution)/shard_map/write40/pallas_call | solution.py:335
  48.2 0.0 collective-permute-done.1.far
  48.2 0.1 add_far.1.fin
  48.3 0.2 collective-permute-start.2
  48.5 1.5 %write120.1 = (bf16[128,640,128]{2,1,0:T(8,128)(2,1)}, bf16[128,640,128]{2,1,0:T(8,128)(2,1)}, bf16[128,640,128]{2,1,0:T(8,128)(2,1)S(1)}, bf16[128,640,128]{2,1,0:T(8,128)(2,1)S(1)}) custom-call(bf16[128,640,128]{2,1,0:T(8,128)(2,1)} %get-tuple-element.49.ko_in, ...), custom_call_target="tpu_custom_call", output_to_operand_aliasing={{0}: (0, {}), {1}: (1, {}), {2}: (2, {}), {3}: (3, {})} | custom-call | flops 800000000 | bytes 2621440 | tf_op jit(solution)/shard_map/write120/pallas_call | solution.py:335
  50.0 0.0 collective-permute-done.2.other
  50.0 0.9 %assemble.1 = bf16[128,2560]{1,0:T(8,128)(2,1)} custom-call(bf16[64,2560]{1,0:T(8,128)(2,1)S(1)} %add_far.1.fin, bf16[64,2560]{1,0:T(8,128)(2,1)S(1)} %collective-permute-done.2.other), custom_call_target="tpu_custom_call" | custom-call | tf_op jit(solution)/shard_map/assemble/pallas_call | solution.py:372
Async XLA Ops:
  34.5 2.3 %collective-permute-start = (bf16[64,2560]{1,0:T(8,128)(2,1)S(1)}, bf16[64,2560]{1,0:T(8,128)(2,1)S(1)}, u32[]{:S(2)}, u32[]{:S(2)}) collective-permute-start(bf16[64,2560]{1,0:T(8,128)(2,1)S(1)} %get-tuple-element.36), channel_id=1, source_target_pairs={{0,1},{1,0},{2,3},{3,2},{4,5},{5,4},{6,7},{7,6},{8,9},{9,8},{10,11... | collective-permute-start | bytes 983048 | tf_op jit(solution)/shard_map/ppermute | solution.py:362
  36.8 11.3 %collective-permute-start.1 = (bf16[64,2560]{1,0:T(8,128)(2,1)S(1)}, bf16[64,2560]{1,0:T(8,128)(2,1)S(1)}, u32[]{:S(2)}, u32[]{:S(2)}) collective-permute-start(bf16[64,2560]{1,0:T(8,128)(2,1)S(1)} %add_near.1.mine), channel_id=1, source_target_pairs={{0,2},{2,0},{1,3},{3,1},{4,6},{6,4},{5,7},{7,5},{8,10},{10,8},{9,1... | collective-permute-start | bytes 983048 | tf_op jit(solution)/shard_map/ppermute | solution.py:366
  48.3 1.7 %collective-permute-start.2 = (bf16[64,2560]{1,0:T(8,128)(2,1)S(1)}, bf16[64,2560]{1,0:T(8,128)(2,1)S(1)}, u32[]{:S(2)}, u32[]{:S(2)}) collective-permute-start(bf16[64,2560]{1,0:T(8,128)(2,1)S(1)} %add_far.1.fin), channel_id=1, source_target_pairs={{0,1},{1,0},{2,3},{3,2},{4,5},{5,4},{6,7},{7,6},{8,9},{9,8},{10,11... | collective-permute-start | bytes 983048 | tf_op jit(solution)/shard_map/ppermute | solution.py:370

commit v6 on v5

--- a/solution.py
+++ b/solution.py
@@ -25,10 +25,11 @@
 NW = D // WCOLS
 WSLOTS = 3
 QROWS = 960
-AHEAD = 3
+AHEAD = 4
 OCOLS = 1280
+OROWS = 8
 HALF_ROWS = ROWS // 2
-CUTS = (32, 40, 120)
+CUTS = (AHEAD * OROWS, 40, 120)
 LIMIT = 22784 << 10
 
 
@@ -40,7 +41,7 @@
     h_sc, min_ = ain, x_ref
 
     def wq_copy(n):
-        rows = pl.ds(n * QROWS, QROWS)
+        rows = pl.ds(n * (QROWS // 2), QROWS // 2)
         return pltpu.make_async_copy(wq_hbm.at[rows], wqbuf.at[rows], wqsem.at[n])
 
     def wo_copy():
@@ -74,7 +75,8 @@
     for c in small:
         c.wait()
     x_copy.wait()
-    wq_copy(1).start()
+    for n in range(1, 4):
+        wq_copy(n).start()
     core = lax.rem(lax.axis_index('tp'), 2)
     mine_rows = pl.ds(pl.multiple_of(core * HALF_ROWS, HALF_ROWS), HALF_ROWS)
     xh_copy = pltpu.make_async_copy(x_hbm.at[mine_rows], xh_ref, xhsem)
@@ -101,7 +103,8 @@
 
     queries = []
     for n in range(3 * KV // QROWS):
-        wq_copy(n).wait()
+        wq_copy(2 * n).wait()
+        wq_copy(2 * n + 1).wait()
         if n == 0:
             kv_start(0)
             w_copy(wu_hbm, 0, 0).start()
@@ -198,6 +201,11 @@
         keep_ref[:, cols] = mine
         acc[:, cols] = near
 
+    def out_copies(j):
+        rows = pl.ds(j * OROWS, OROWS)
+        return [pltpu.make_async_copy(src.at[rows], dst.at[rows], outsem.at[n, j])
+                for n, (src, dst) in enumerate(((kbuf, ko_hbm), (vbuf, vo_hbm)))]
+
     s_sc[...] = jnp.zeros_like(s_sc)
     p_sc[...] = jnp.zeros_like(p_sc)
 
@@ -226,6 +234,9 @@
         attend(i)
         if more:
             kv_start(i + AHEAD)
+        else:
+            for c in out_copies(i - (NBLK - AHEAD)):
+                c.start()
         return 0
 
     lax.fori_loop(0, NW - WSLOTS, functools.partial(up_body, wu_hbm, 0), 0)
@@ -233,13 +244,6 @@
     lax.fori_loop(0, NW - WSLOTS, functools.partial(down_body, True), 0)
     lax.fori_loop(NW - WSLOTS, NW, functools.partial(down_body, False), 0)
     wo_copy().start()
-    outs = []
-    for n, (src, dst) in enumerate(((kbuf, ko_hbm), (vbuf, vo_hbm))):
-        for r in range(0, CUTS[0], BLK):
-            rows = pl.ds(r, BLK)
-            outs.append(pltpu.make_async_copy(src.at[rows], dst.at[rows], outsem.at[n, r // BLK]))
-    for c in outs:
-        c.start()
     lax.fori_loop(2 * NW, NBLK - AHEAD, functools.partial(rest_body, True), 0)
     lax.fori_loop(NBLK - AHEAD, NBLK, functools.partial(rest_body, False), 0)
     wo_copy().wait()
@@ -254,8 +258,9 @@
         keep_ref[:, cols] += mine
         send_ref[:, cols] = (acc[:, cols] + near).astype(bf16)
     xh_copy.wait()
-    for c in outs:
-        c.wait()
+    for j in range(AHEAD):
+        for c in out_copies(j):
+            c.wait()
 
 
 def add_near(keep, near, mine):
@@ -324,7 +329,7 @@
             pltpu.VMEM((ROWS, KV), f32), pltpu.VMEM((KV, ROWS), bf16), pltpu.VMEM((KV, ROWS), bf16),
             pltpu.VMEM((HALF_ROWS, D), f32), pltpu.VMEM((ROWS, KV), f32),
             pltpu.VMEM((BLK * 8, SEQ), f32), pltpu.VMEM((BLK * 8, SEQ), f32),
-            dma((NBLK,)), dma((NBLK,)), dma((3 * KV // QROWS,)), dma((WSLOTS,)), dma, dma, dma, dma((7,)), dma((2, CUTS[0] // BLK)),
+            dma((NBLK,)), dma((NBLK,)), dma((6 * KV // QROWS,)), dma((WSLOTS,)), dma, dma, dma, dma((7,)), dma((2, AHEAD)),
         ],
         compiler_params=pltpu.CompilerParams(vmem_limit_bytes=LIMIT),
         cost_estimate=pl.CostEstimate(flops=5 * 10**9, bytes_accessed=8 * 10**7, transcendentals=0),

time: 51 us -> 47.4 us (0.929)
  Pallas kernels: 46.6 us -> 42.9 us
    pallas_call x1, Pallas kernels: 33.8 us -> 30.1 us  [device_step(): main(positions, positions.reshape(1, ROWS), jnp.asarray(inv_tab), ga, ba,...]
  transfers between devices with their start and end apart: 3 -> 3, of which waited for: 0 -> 0; matrix products, arithmetic and copies ran while one was open for 0% -> 0% of each run, Pallas kernels for 23% -> 25%
where the time goes in v6:
time: 47.4 us; the launch traced here: 47.2 us
  Pallas kernels  42.9 us (91%)
  starting transfers between devices  3.57 us (8%)
  between operations  0.71 us (1%)
    pallas_call x1, Pallas kernels, device_step(): main(positions, positions.reshape(1, ROWS), jnp.asarray(inv_tab), ga, ba,...  30.1 us
    pallas_call x3, Pallas kernels, writer(): pl.pallas_call(functools.partial(writer_kernel, first, last, len(carry)),...  11.7 us
    ppermute x1, starting transfers between devices, device_step(): far = lax.ppermute(mine, 'tp', far_pairs)  2.63 us
  transfers between devices with their start and end apart: 3, of which 0 were waited for; matrix products, arithmetic and copies ran while one was open for 0% of the time, Pallas kernels for 25%

profile of v6, /device:TPU:0, one launch (start us, length us, event | category | flops | bytes accessed | tf_op | source)
XLA Modules:
  0.0 47.2 jit_solution(16400465205614219071)
XLA Ops:
  0.6 30.1 %layer.1 = (bf16[128,640,128]{2,1,0:T(8,128)(2,1)}, bf16[128,640,128]{2,1,0:T(8,128)(2,1)}, bf16[128,640,128]{2,1,0:T(8,128)(2,1)S(1)}, bf16[128,640,128]{2,1,0:...) custom-call(s32[128]{0:T(128)} %pos_hbm.1, ...), custom_call_target="tpu_custom_call" | custom-call | flops 5000000000 | bytes 80000000 | tf_op jit(solution)/shard_map/layer/pallas_call | solution.py:365
  30.8 0.8 %collective-permute-start = (bf16[64,2560]{1,0:T(8,128)(2,1)S(1)}, bf16[64,2560]{1,0:T(8,128)(2,1)S(1)}, u32[]{:S(2)}, u32[]{:S(2)}) collective-permute-start(bf16[64,2560]{1,0:T(8,128)(2,1)S(1)} %get-tuple-element.36), channel_id=1, source_target_pairs={{0,1},{1,0},{2,3},{3,2},{4,5},{5,4},{6,7},{7,6},{8,9},{9,8},{10,11... | collective-permute-start | bytes 983048 | tf_op jit(solution)/shard_map/ppermute | solution.py:367
  31.6 1.5 %write32.1 = (bf16[128,640,128]{2,1,0:T(8,128)(2,1)}, bf16[128,640,128]{2,1,0:T(8,128)(2,1)}, bf16[128,640,128]{2,1,0:T(8,128)(2,1)S(1)}, bf16[128,640,128]{2,1,...) custom-call(bf16[128,640,128]{2,1,0:T(8,128)(2,1)} %get-tuple-elemen, ...), custom_call_target="tpu_custom_call", output_to_operand_aliasing={{0}: (0, {}), {1}: (1, {}), {2}: (2, {}), {3}: (3, {}), {4}... | custom-call | flops 800000000 | bytes 2621440 | tf_op jit(solution)/shard_map/write32/pallas_call | solution.py:340
  33.1 0.0 collective-permute-done.near
  33.1 0.1 add_near.1.mine
  33.1 2.6 %collective-permute-start.1 = (bf16[64,2560]{1,0:T(8,128)(2,1)S(1)}, bf16[64,2560]{1,0:T(8,128)(2,1)S(1)}, u32[]{:S(2)}, u32[]{:S(2)}) collective-permute-start(bf16[64,2560]{1,0:T(8,128)(2,1)S(1)} %add_near.1.mine), channel_id=1, source_target_pairs={{0,2},{2,0},{1,3},{3,1},{4,6},{6,4},{5,7},{7,5},{8,10},{10,8},{9,1... | collective-permute-start | bytes 983048 | tf_op jit(solution)/shard_map/ppermute | solution.py:371
  35.8 8.7 %write40.1 = (bf16[128,640,128]{2,1,0:T(8,128)(2,1)}, bf16[128,640,128]{2,1,0:T(8,128)(2,1)}, bf16[128,640,128]{2,1,0:T(8,128)(2,1)S(1)}, bf16[128,640,128]{2,1,0:T(8,128)(2,1)S(1)}, bf16[64,2560]{1,0:T(8,128)(2,1)S(1)}) custom-call(bf16[128,640,128]{2,1,0:T(8,128)(2,1)} %get-tuple-elemen, ...), custom_call_target="tpu_custom_call", output_to_operand_aliasing={{0}: (0, {}), {1}: (1, {}), {2}: (2, {}), {3}: (3, {}), {4}... | custom-call | flops 8000000000 | bytes 26214400 | tf_op jit(solution)/shard_map/write40/pallas_call | solution.py:340
  44.5 0.0 collective-permute-done.1.far
  44.5 0.1 add_far.1.fin
  44.6 0.2 collective-permute-start.2
  44.8 1.5 %write120.1 = (bf16[128,640,128]{2,1,0:T(8,128)(2,1)}, bf16[128,640,128]{2,1,0:T(8,128)(2,1)}, bf16[128,640,128]{2,1,0:T(8,128)(2,1)S(1)}, bf16[128,640,128]{2,1,0:T(8,128)(2,1)S(1)}) custom-call(bf16[128,640,128]{2,1,0:T(8,128)(2,1)} %get-tuple-element.49.ko_in, ...), custom_call_target="tpu_custom_call", output_to_operand_aliasing={{0}: (0, {}), {1}: (1, {}), {2}: (2, {}), {3}: (3, {})} | custom-call | flops 800000000 | bytes 2621440 | tf_op jit(solution)/shard_map/write120/pallas_call | solution.py:340
  46.3 0.0 collective-permute-done.2.other
  46.3 0.9 %assemble.1 = bf16[128,2560]{1,0:T(8,128)(2,1)} custom-call(bf16[64,2560]{1,0:T(8,128)(2,1)S(1)} %add_far.1.fin, bf16[64,2560]{1,0:T(8,128)(2,1)S(1)} %collective-permute-done.2.other), custom_call_target="tpu_custom_call" | custom-call | tf_op jit(solution)/shard_map/assemble/pallas_call | solution.py:377
Async XLA Ops:
  30.8 2.3 %collective-permute-start = (bf16[64,2560]{1,0:T(8,128)(2,1)S(1)}, bf16[64,2560]{1,0:T(8,128)(2,1)S(1)}, u32[]{:S(2)}, u32[]{:S(2)}) collective-permute-start(bf16[64,2560]{1,0:T(8,128)(2,1)S(1)} %get-tuple-element.36), channel_id=1, source_target_pairs={{0,1},{1,0},{2,3},{3,2},{4,5},{5,4},{6,7},{7,6},{8,9},{9,8},{10,11... | collective-permute-start | bytes 983048 | tf_op jit(solution)/shard_map/ppermute | solution.py:367
  33.1 11.3 %collective-permute-start.1 = (bf16[64,2560]{1,0:T(8,128)(2,1)S(1)}, bf16[64,2560]{1,0:T(8,128)(2,1)S(1)}, u32[]{:S(2)}, u32[]{:S(2)}) collective-permute-start(bf16[64,2560]{1,0:T(8,128)(2,1)S(1)} %add_near.1.mine), channel_id=1, source_target_pairs={{0,2},{2,0},{1,3},{3,1},{4,6},{6,4},{5,7},{7,5},{8,10},{10,8},{9,1... | collective-permute-start | bytes 983048 | tf_op jit(solution)/shard_map/ppermute | solution.py:371
  44.6 1.7 %collective-permute-start.2 = (bf16[64,2560]{1,0:T(8,128)(2,1)S(1)}, bf16[64,2560]{1,0:T(8,128)(2,1)S(1)}, u32[]{:S(2)}, u32[]{:S(2)}) collective-permute-start(bf16[64,2560]{1,0:T(8,128)(2,1)S(1)} %add_far.1.fin), channel_id=1, source_target_pairs={{0,1},{1,0},{2,3},{3,2},{4,5},{5,4},{6,7},{7,6},{8,9},{9,8},{10,11... | collective-permute-start | bytes 983048 | tf_op jit(solution)/shard_map/ppermute | solution.py:375

commit v7 on v6

--- a/solution.py
+++ b/solution.py
@@ -231,12 +231,12 @@
 
     def rest_body(more, i, _):
         arrive(i)
-        attend(i)
         if more:
             kv_start(i + AHEAD)
         else:
             for c in out_copies(i - (NBLK - AHEAD)):
                 c.start()
+        attend(i)
         return 0
 
     lax.fori_loop(0, NW - WSLOTS, functools.partial(up_body, wu_hbm, 0), 0)

time: 47.4 us -> 49.3 us (1.040)
  Pallas kernels: 42.9 us -> 44.8 us
    pallas_call x1, Pallas kernels: 30.1 us -> 32 us  [device_step(): main(positions, positions.reshape(1, ROWS), jnp.asarray(inv_tab), ga, ba,...]
  transfers between devices with their start and end apart: 3 -> 3, of which waited for: 0 -> 0; matrix products, arithmetic and copies ran while one was open for 0% -> 0% of each run, Pallas kernels for 25% -> 24%
where the time goes in v7:
time: 49.3 us; the launch traced here: 49.1 us
  Pallas kernels  44.8 us (91%)
  starting transfers between devices  3.57 us (7%)
  between operations  0.71 us (1%)
    pallas_call x1, Pallas kernels, device_step(): main(positions, positions.reshape(1, ROWS), jnp.asarray(inv_tab), ga, ba,...  32 us
    pallas_call x3, Pallas kernels, writer(): pl.pallas_call(functools.partial(writer_kernel, first, last, len(carry)),...  11.7 us
    ppermute x1, starting transfers between devices, device_step(): far = lax.ppermute(mine, 'tp', far_pairs)  2.63 us
  transfers between devices with their start and end apart: 3, of which 0 were waited for; matrix products, arithmetic and copies ran while one was open for 0% of the time, Pallas kernels for 24%

profile of v7, /device:TPU:0, one launch (start us, length us, event | category | flops | bytes accessed | tf_op | source)
XLA Modules:
  0.0 49.1 jit_solution(4782138187677080659)
XLA Ops:
  0.6 32.0 %layer.1 = (bf16[128,640,128]{2,1,0:T(8,128)(2,1)}, bf16[128,640,128]{2,1,0:T(8,128)(2,1)}, bf16[128,640,128]{2,1,0:T(8,128)(2,1)S(1)}, bf16[128,640,128]{2,1,0:...) custom-call(s32[128]{0:T(128)} %pos_hbm.1, ...), custom_call_target="tpu_custom_call" | custom-call | flops 5000000000 | bytes 80000000 | tf_op jit(solution)/shard_map/layer/pallas_call | solution.py:365
  32.7 0.8 %collective-permute-start = (bf16[64,2560]{1,0:T(8,128)(2,1)S(1)}, bf16[64,2560]{1,0:T(8,128)(2,1)S(1)}, u32[]{:S(2)}, u32[]{:S(2)}) collective-permute-start(bf16[64,2560]{1,0:T(8,128)(2,1)S(1)} %get-tuple-element.36), channel_id=1, source_target_pairs={{0,1},{1,0},{2,3},{3,2},{4,5},{5,4},{6,7},{7,6},{8,9},{9,8},{10,11... | collective-permute-start | bytes 983048 | tf_op jit(solution)/shard_map/ppermute | solution.py:367
  33.5 1.5 %write32.1 = (bf16[128,640,128]{2,1,0:T(8,128)(2,1)}, bf16[128,640,128]{2,1,0:T(8,128)(2,1)}, bf16[128,640,128]{2,1,0:T(8,128)(2,1)S(1)}, bf16[128,640,128]{2,1,...) custom-call(bf16[128,640,128]{2,1,0:T(8,128)(2,1)} %get-tuple-elemen, ...), custom_call_target="tpu_custom_call", output_to_operand_aliasing={{0}: (0, {}), {1}: (1, {}), {2}: (2, {}), {3}: (3, {}), {4}... | custom-call | flops 800000000 | bytes 2621440 | tf_op jit(solution)/shard_map/write32/pallas_call | solution.py:340
  35.0 0.0 collective-permute-done.near
  35.0 0.1 add_near.1.mine
  35.0 2.6 %collective-permute-start.1 = (bf16[64,2560]{1,0:T(8,128)(2,1)S(1)}, bf16[64,2560]{1,0:T(8,128)(2,1)S(1)}, u32[]{:S(2)}, u32[]{:S(2)}) collective-permute-start(bf16[64,2560]{1,0:T(8,128)(2,1)S(1)} %add_near.1.mine), channel_id=1, source_target_pairs={{0,2},{2,0},{1,3},{3,1},{4,6},{6,4},{5,7},{7,5},{8,10},{10,8},{9,1... | collective-permute-start | bytes 983048 | tf_op jit(solution)/shard_map/ppermute | solution.py:371
  37.7 8.7 %write40.1 = (bf16[128,640,128]{2,1,0:T(8,128)(2,1)}, bf16[128,640,128]{2,1,0:T(8,128)(2,1)}, bf16[128,640,128]{2,1,0:T(8,128)(2,1)S(1)}, bf16[128,640,128]{2,1,0:T(8,128)(2,1)S(1)}, bf16[64,2560]{1,0:T(8,128)(2,1)S(1)}) custom-call(bf16[128,640,128]{2,1,0:T(8,128)(2,1)} %get-tuple-elemen, ...), custom_call_target="tpu_custom_call", output_to_operand_aliasing={{0}: (0, {}), {1}: (1, {}), {2}: (2, {}), {3}: (3, {}), {4}... | custom-call | flops 8000000000 | bytes 26214400 | tf_op jit(solution)/shard_map/write40/pallas_call | solution.py:340
  46.4 0.0 collective-permute-done.1.far
  46.4 0.1 add_far.1.fin
  46.5 0.2 collective-permute-start.2
  46.7 1.5 %write120.1 = (bf16[128,640,128]{2,1,0:T(8,128)(2,1)}, bf16[128,640,128]{2,1,0:T(8,128)(2,1)}, bf16[128,640,128]{2,1,0:T(8,128)(2,1)S(1)}, bf16[128,640,128]{2,1,0:T(8,128)(2,1)S(1)}) custom-call(bf16[128,640,128]{2,1,0:T(8,128)(2,1)} %get-tuple-element.49.ko_in, ...), custom_call_target="tpu_custom_call", output_to_operand_aliasing={{0}: (0, {}), {1}: (1, {}), {2}: (2, {}), {3}: (3, {})} | custom-call | flops 800000000 | bytes 2621440 | tf_op jit(solution)/shard_map/write120/pallas_call | solution.py:340
  48.2 0.0 collective-permute-done.2.other
  48.2 0.9 %assemble.1 = bf16[128,2560]{1,0:T(8,128)(2,1)} custom-call(bf16[64,2560]{1,0:T(8,128)(2,1)S(1)} %add_far.1.fin, bf16[64,2560]{1,0:T(8,128)(2,1)S(1)} %collective-permute-done.2.other), custom_call_target="tpu_custom_call" | custom-call | tf_op jit(solution)/shard_map/assemble/pallas_call | solution.py:377
Async XLA Ops:
  32.7 2.3 %collective-permute-start = (bf16[64,2560]{1,0:T(8,128)(2,1)S(1)}, bf16[64,2560]{1,0:T(8,128)(2,1)S(1)}, u32[]{:S(2)}, u32[]{:S(2)}) collective-permute-start(bf16[64,2560]{1,0:T(8,128)(2,1)S(1)} %get-tuple-element.36), channel_id=1, source_target_pairs={{0,1},{1,0},{2,3},{3,2},{4,5},{5,4},{6,7},{7,6},{8,9},{9,8},{10,11... | collective-permute-start | bytes 983048 | tf_op jit(solution)/shard_map/ppermute | solution.py:367
  35.0 11.3 %collective-permute-start.1 = (bf16[64,2560]{1,0:T(8,128)(2,1)S(1)}, bf16[64,2560]{1,0:T(8,128)(2,1)S(1)}, u32[]{:S(2)}, u32[]{:S(2)}) collective-permute-start(bf16[64,2560]{1,0:T(8,128)(2,1)S(1)} %add_near.1.mine), channel_id=1, source_target_pairs={{0,2},{2,0},{1,3},{3,1},{4,6},{6,4},{5,7},{7,5},{8,10},{10,8},{9,1... | collective-permute-start | bytes 983048 | tf_op jit(solution)/shard_map/ppermute | solution.py:371
  46.5 1.7 %collective-permute-start.2 = (bf16[64,2560]{1,0:T(8,128)(2,1)S(1)}, bf16[64,2560]{1,0:T(8,128)(2,1)S(1)}, u32[]{:S(2)}, u32[]{:S(2)}) collective-permute-start(bf16[64,2560]{1,0:T(8,128)(2,1)S(1)} %add_far.1.fin), channel_id=1, source_target_pairs={{0,1},{1,0},{2,3},{3,2},{4,5},{5,4},{6,7},{7,6},{8,9},{9,8},{10,11... | collective-permute-start | bytes 983048 | tf_op jit(solution)/shard_map/ppermute | solution.py:375
